TPU v7x, 32 devices: a whole 2x2x4 slice. The times are simulated.
32 devices in a mesh: dp: 2 (over x), tx: 4 (over z), ty: 4 (over y, core).
Axes of the slice: x: 2, y: 2, z: 4, core: 2. Of those that a mesh axis runs over, the one named last changes fastest.
Arguments:
- x_act: bfloat16 [24, 768, 1024], P('dp', None, 'tx'), parts along dimension 0
- cot_out: bfloat16 [24, 768, 1024], P('dp', None, 'tx'), parts along dimension 0
- ln1_gain: bfloat16 [1024], P('tx')
- ln1_bias: bfloat16 [1024], P('tx')
- ln2_gain: bfloat16 [1024], P('tx')
- ln2_bias: bfloat16 [1024], P('tx')
- w_qkv: bfloat16 [1024, 16, 192], P('tx', 'ty')
- b_qkv: bfloat16 [16, 192], P('ty')
- w_dense: bfloat16 [1024, 1024], P('ty', 'tx')
- b_dense: bfloat16 [1024], P('tx')
- w_up: bfloat16 [1024, 4096], P('tx', 'ty')
- b_up: bfloat16 [4096], P('ty')
- w_down: bfloat16 [4096, 1024], P('ty', 'tx')
- b_down: bfloat16 [1024], P('tx')
Outputs:
- output 1: bfloat16 [24, 768, 1024], P('dp', None, 'tx'), parts along dimension 0
- output 2: bfloat16 [24, 768, 1024], P('dp', None, 'tx'), parts along dimension 0
- output 3: float32 [2048], P(('dp', 'tx')), parts along dimension 0
- output 4: float32 [2048], P(('dp', 'tx')), parts along dimension 0
- output 5: float32 [2048], P(('dp', 'tx')), parts along dimension 0
- output 6: float32 [2048], P(('dp', 'tx')), parts along dimension 0
- output 7: float32 [2048, 16, 192], P(('dp', 'tx'), 'ty'), parts along dimension 0
- output 8: float32 [32, 192], P(('dp', 'ty')), parts along dimension 0
- output 9: float32 [2048, 1024], P(('dp', 'ty'), 'tx'), parts along dimension 0
- output 10: float32 [2048], P(('dp', 'tx')), parts along dimension 0
- output 11: float32 [2048, 4096], P(('dp', 'tx'), 'ty'), parts along dimension 0
- output 12: float32 [8192], P(('dp', 'ty')), parts along dimension 0
- output 13: float32 [8192, 1024], P(('dp', 'ty'), 'tx'), parts along dimension 0
- output 14: float32 [2048], P(('dp', 'tx')), parts along dimension 0
There are 2 independent parts. A program takes and returns all parts, laid end to end along the dimension named above; an argument that names none is the same for every part.
All inputs are finite; a program needn't handle non-finite values.
Results may differ from a plain program's by a relative error of at most 0.02.
Values are sent between devices in bfloat16 or wider.
A program may use at most 1 GiB of HBM per device.

v0:
```python
import functools
import jax
import jax.numpy as jnp
from jax import lax
from jax.experimental import pallas as pl
from jax.experimental.pallas import tpu as pltpu
from jax.sharding import PartitionSpec as P

LN_EPS = 1e-5
ROPE_BASE = 10000.0
HEAD = 64
ROT = 16
F32 = jnp.float32
BF16 = jnp.bfloat16

def rope_tables(seq_len, width):
    inv_freq = ROPE_BASE ** (-jnp.arange(0, ROT, 2, dtype=F32) / ROT)
    angles = jnp.arange(seq_len, dtype=F32)[:, None] * inv_freq[None, :]
    angles = jnp.concatenate([angles, angles], axis=-1)
    pad = ((0, 0), (0, HEAD - ROT))
    cos_head = jnp.pad(jnp.cos(angles), pad, constant_values=1.0)
    sin_head = jnp.pad(jnp.sin(angles), pad)
    return jnp.tile(cos_head, (1, width // HEAD)), jnp.tile(sin_head, (1, width // HEAD))


def rope_turn(width):
    row = lax.broadcasted_iota(jnp.int32, (width, width), 0)
    col = lax.broadcasted_iota(jnp.int32, (width, width), 1)
    lane = col % HEAD
    minus = (row == col + ROT // 2) & (lane < ROT // 2)
    plus = (row == col - ROT // 2) & (lane >= ROT // 2) & (lane < ROT)
    return (plus.astype(F32) - minus.astype(F32)).astype(BF16)


def dot_nn(a, b):
    return lax.dot_general(a, b, (((1,), (0,)), ((), ())), preferred_element_type=F32)


def dot_nt(a, b):
    return lax.dot_general(a, b, (((1,), (1,)), ((), ())), preferred_element_type=F32)


def dot_tn(a, b):
    return lax.dot_general(a, b, (((0,), (0,)), ((), ())), preferred_element_type=F32)


MESH = pl.DeviceIdType.MESH
BOTH = range(2)
OTHERS = (1, 3, 2)


def block(i, size):
    return pl.ds(pl.multiple_of(i * size, size), size)


def row_mean(v):
    return jnp.mean(v, axis=-1, keepdims=True)


def normalise(v):
    mean = row_mean(v)
    inv_std = lax.rsqrt(row_mean(v * v) - mean * mean + LN_EPS)
    return (v - mean) * inv_std, inv_std


def fold(v):
    return v.reshape(v.shape[0] // 8, 8, v.shape[1]).sum(0)


class Links:
    def __init__(self, send_sems, recv_sems):
        self.send_sems, self.recv_sems, self.count = send_sems, recv_sems, 0

    def slot(self, count=1):
        self.count += count
        return self.count - count

    def make(self, slot, src, dst, dev):
        return pltpu.make_async_remote_copy(src_ref=src, dst_ref=dst, send_sem=self.send_sems.at[slot], recv_sem=self.recv_sems.at[slot], device_id=dev, device_id_type=MESH)

    def send(self, slot, src, dst, dev, cond=None):
        def go():
            self.make(slot, src, dst, dev).start()
        go() if cond is None else pl.when(cond)(go)

    def arrive(self, slot, dst, dev, cond=None):
        def go():
            self.make(slot, dst, dst, dev).wait_recv()
        go() if cond is None else pl.when(cond)(go)

    def sent(self, slot, like, cond=None):
        def go():
            self.make(slot, like, like, (0, 0, 0)).wait_send()
        go() if cond is None else pl.when(cond)(go)


def neighbours():
    g, z, t = lax.axis_index('dp'), lax.axis_index('tx'), lax.axis_index('ty')
    core, y = t % 2, t // 2
    t_core, t_y, t_diag = y * 2 + 1 - core, (1 - y) * 2 + core, (1 - y) * 2 + 1 - core
    return g, z, t, core, y, t_core, t_y, t_diag


def enter(devices):
    barrier = pltpu.get_barrier_semaphore()
    for dev in devices:
        pl.semaphore_signal(barrier, inc=1, device_id=dev, device_id_type=MESH)
    pl.semaphore_wait(barrier, len(devices))


def front_kernel(
    x_in, c_in, wu_in, wd_in, wa_in, v_in, b_qkv, b_up,
    x_out, c_out, wu_out, wd_out, wa_out, v_out, h1_out, qkv_out, u_out, dpre_out, dctx_out, dwd_out, dwu_out, dbup_out,
    x_v, c_v, wu_v, wd_v, wa_v, h1_v, h2_v, u_v, gp_v, qkv_v, dpre_v, dctx_v, dw_v,
    send_sems, recv_sems, local_sems, out_sems, *, n_tx, n_ty, blk,
):
    g, z, t, core, y, t_core, t_y, t_diag = neighbours()
    core_dev, y_dev, x_dev = (g, z, t_core), (g, z, t_y), (1 - g, z, t)
    z_dev = [(g, (z + k) % n_tx, t) for k in range(n_tx)]
    left, right = (g, z - 1, t), (g, z + 1, t)
    d_loc = x_in.shape[-1]
    half = d_loc // 2
    tok = x_v.shape[0]
    chunk = tok // n_ty
    width = dctx_v.shape[-1]
    links = Links(send_sems, recv_sems)

    def cols(s):
        return block(s, d_loc)

    def rows(c):
        return block(c, chunk)

    def w_rows(s, group):
        return pl.ds(pl.multiple_of(s * d_loc + group * half, half), half)

    own = [pltpu.make_async_copy(v_in, v_out.at[:, cols(z)], local_sems.at[0])]
    for i, (src, dst) in enumerate(((wu_in, wu_v), (wa_in, wa_v), (wd_in, wd_v))):
        own.append(pltpu.make_async_copy(src, dst.at[cols(z), :], local_sems.at[1 + i]))
    for i, (src, dst) in enumerate(((x_in, x_v), (c_in, c_v))):
        for c in range(n_ty):
            own.append(pltpu.make_async_copy(src.at[z, c], dst.at[pl.ds(c * chunk, chunk), cols(z)], local_sems.at[4 + i * n_ty + c]))
    for copy in own:
        copy.start()
    enter([core_dev, y_dev, x_dev] + z_dev[1:])

    weights = ((wu_in, wu_v), (wa_in, wa_v), (wd_in, wd_v))
    w_slot = [[links.slot() for _ in range(2 * n_tx)] for _ in weights]
    x_slot = [[links.slot() for _ in range(n_tx)] for _ in weights]

    def w_send(w, hops, src):
        s_left, s_right = z - hops, z + hops
        links.send(w_slot[w][hops + 1], src(s_left), weights[w][1].at[w_rows(s_left, g), :], right, (s_left >= 0) & (z < n_tx - 1))
        links.send(w_slot[w][n_tx + hops + 1], src(s_right), weights[w][1].at[w_rows(s_right, g), :], left, (s_right < n_tx) & (z > 0))

    def w_start(w):
        mine = weights[w][0].at[block(g, half), :]
        w_send(w, 0, lambda s: mine)

    def w_sides(hops):
        return (hops, hops, z - hops, z - hops >= 0), (n_tx + hops, n_tx - hops, z + hops, z + hops < n_tx)

    def w_pass(w, hops):
        out = weights[w][1]
        for slot, x_at, s, ok in w_sides(hops):
            place = out.at[w_rows(s, g), :]
            links.arrive(w_slot[w][slot], place, right, ok)
            links.send(x_slot[w][x_at], place, place, x_dev, ok)
        if hops < n_tx - 1:
            w_send(w, hops, lambda s: out.at[w_rows(s, g), :])

    def w_finish(w):
        for hops in OTHERS:
            for slot, x_at, s, ok in w_sides(hops):
                links.arrive(x_slot[w][x_at], weights[w][1].at[w_rows(s, 1 - g), :], x_dev, ok)

    arrays = ((x_in, x_v), (c_in, c_v))
    z_slot = [[links.slot() for _ in range(n_tx)] for _ in arrays]
    y_slot = [[links.slot() for _ in range(n_tx)] for _ in arrays]
    c_slot = [[[links.slot() for _ in BOTH] for _ in range(n_tx)] for _ in arrays]
    v_slot = [links.slot() for _ in range(n_tx)]

    def src_cols(k):
        return cols((z + n_tx - k) % n_tx)

    def t_start(a):
        for k in OTHERS:
            links.send(z_slot[a][k], arrays[a][0].at[(z + k) % n_tx, t], arrays[a][1].at[rows(t), cols(z)], z_dev[k])

    def t_pass(a, k):
        place = arrays[a][1].at[rows(t), src_cols(k)]
        links.arrive(z_slot[a][k], place, y_dev)
        links.send(y_slot[a][k], place, place, y_dev)
        links.send(c_slot[a][k][0], place, place, core_dev)

    def t_pass_y(a, k):
        place = arrays[a][1].at[rows(t_y), src_cols(k)]
        links.arrive(y_slot[a][k], place, y_dev)
        links.send(c_slot[a][k][1], place, place, core_dev)

    def t_finish(a):
        for k in OTHERS:
            for j, c in enumerate((t_core, t_diag)):
                links.arrive(c_slot[a][k][j], arrays[a][1].at[rows(c), src_cols(k)], core_dev)

    w_start(0)
    w_start(1)
    for k in OTHERS:
        links.send(v_slot[k], v_in, v_out.at[:, cols(z)], z_dev[k])
    t_start(0)
    w_pass(0, 1)
    w_pass(1, 1)
    for k in OTHERS:
        t_pass(0, k)
    w_pass(0, 2)
    w_pass(1, 2)
    w_start(2)
    t_start(1)
    for k in OTHERS:
        t_pass_y(0, k)
    w_pass(0, 3)
    w_pass(1, 3)
    w_finish(0)
    w_finish(1)
    t_finish(0)
    for k in OTHERS:
        links.arrive(v_slot[k], v_out.at[:, src_cols(k)], y_dev)
    for copy in own:
        copy.wait()

    outputs = []

    def write(src, dst):
        copy = pltpu.make_async_copy(src, dst, out_sems.at[len(outputs)])
        copy.start()
        outputs.append(copy)

    write(x_v, x_out)
    write(wu_v, wu_out)
    write(wa_v, wa_out)
    late_steps = {
        0: lambda: w_pass(2, 1),
        2: lambda: [t_pass(1, k) for k in OTHERS],
        3: lambda: w_pass(2, 2),
        4: lambda: [t_pass_y(1, k) for k in OTHERS],
        6: lambda: w_pass(2, 3),
    }
    vec = v_out[...].astype(F32)

    def forward(i, carry):
        at = block(i, blk)
        xf = x_v[at, :].astype(F32)
        xh, _ = normalise(xf)
        h1 = (xh * vec[0:1] + vec[1:2]).astype(BF16)
        h2 = (xh * vec[2:3] + vec[3:4]).astype(BF16)
        h1_v[at, :] = h1
        h2_v[at, :] = h2
        qkv_v[at, :] = (dot_nn(h1, wa_v[:, :3 * width]) + b_qkv[0:1, :]).astype(BF16)
        pre = (dot_nn(h2, wu_v[...]) + b_up[0:1, :]).astype(BF16).astype(F32)
        cdf = 0.5 * (1.0 + lax.erf(pre * (0.5 ** 0.5)))
        u_v[at, :] = (pre * cdf).astype(BF16)
        gp_v[at, :] = cdf + pre * (jnp.exp(-0.5 * pre * pre) * (1.0 / (2.0 * jnp.pi) ** 0.5))
        for when, what in late_steps.items():
            pl.when(i == when)(lambda: (what(), None)[1])
        return carry

    lax.fori_loop(0, tok // blk, forward, 0)
    write(h1_v, h1_out)
    write(qkv_v, qkv_out)
    write(u_v, u_out)
    w_finish(2)
    t_finish(1)
    write(c_v, c_out)
    write(wd_v, wd_out)
    dbup_out[...] = jnp.zeros_like(dbup_out)

    def backward(i, carry):
        at = block(i, blk)
        cot = c_v[at, :]
        d_gelu = dot_nn(cot, wd_v[...]).astype(BF16).astype(F32)
        d_pre = (d_gelu * gp_v[at, :]).astype(BF16)
        dpre_v[at, :] = d_pre
        dbup_out[...] += fold(d_pre.astype(F32))
        dctx_v[at, :] = dot_nn(cot, wa_v[:, 3 * width:]).astype(BF16)
        return carry

    lax.fori_loop(0, tok // blk, backward, 0)
    write(dpre_v, dpre_out)
    write(dctx_v, dctx_out)
    for i, (lhs, rhs, out) in enumerate(((c_v, u_v, dwd_out), (h2_v, dpre_v, dwu_out))):
        def weight(r, carry):
            dw_v[i, cols(r), :] = dot_tn(lhs[:, cols(r)], rhs[...]).astype(BF16)
            return carry
        lax.fori_loop(0, n_tx, weight, 0)
        write(dw_v.at[i], out)
    piece = x_v.at[pl.ds(0, chunk), pl.ds(0, d_loc)]
    for a in BOTH:
        for k in OTHERS:
            for slot in (z_slot[a][k], y_slot[a][k], *c_slot[a][k]):
                links.sent(slot, piece)
    for w in range(len(weights)):
        shard = weights[w][1].at[pl.ds(0, half), :]
        for hops in range(n_tx):
            if hops:
                for _, x_at, _, ok in w_sides(hops):
                    links.sent(x_slot[w][x_at], shard, ok)
            if hops < n_tx - 1:
                links.sent(w_slot[w][hops + 1], shard, (z - hops >= 0) & (z < n_tx - 1))
                links.sent(w_slot[w][n_tx + hops + 1], shard, (z + hops < n_tx) & (z > 0))
    for k in OTHERS:
        links.sent(v_slot[k], v_in)
    for copy in outputs:
        copy.wait()


def layer_front(x_act, cot_out, w_up, w_dt, w_a, vecs, b_qkv, b_up, n_tx, n_ty):
    batch, seq, d_loc = x_act.shape
    tok = batch * seq // n_tx
    d_model, ff, width, blk = d_loc * n_tx, w_up.shape[1], b_qkv.shape[1] // 3, 256
    any_spec, vmem = pl.BlockSpec(memory_space=pl.ANY), pl.BlockSpec(memory_space=pltpu.VMEM)
    arr = lambda *shape: jax.ShapeDtypeStruct(shape, BF16)
    buf = lambda *shape: pltpu.VMEM(shape, BF16)
    slots = 3 * 3 * n_tx + 2 * 4 * n_tx + n_tx
    split = lambda a: a.reshape(n_tx, n_ty, tok // n_ty, d_loc)
    return pl.pallas_call(
        functools.partial(front_kernel, n_tx=n_tx, n_ty=n_ty, blk=blk),
        in_specs=[any_spec] * 6 + [vmem] * 2,
        out_specs=[any_spec] * 5 + [vmem] + [any_spec] * 7 + [vmem],
        out_shape=[
            arr(tok, d_model), arr(tok, d_model), arr(d_model, ff), arr(d_model, ff), arr(d_model, 4 * width), arr(vecs.shape[0], d_model),
            arr(tok, d_model), arr(tok, 3 * width), arr(tok, ff), arr(tok, ff), arr(tok, width), arr(d_model, ff), arr(d_model, ff),
            jax.ShapeDtypeStruct((8, ff), F32),
        ],
        scratch_shapes=[
            buf(tok, d_model), buf(tok, d_model), buf(d_model, ff), buf(d_model, ff), buf(d_model, 4 * width),
            buf(tok, d_model), buf(tok, d_model), buf(tok, ff), pltpu.VMEM((tok, ff), F32), buf(tok, 3 * width), buf(tok, ff), buf(tok, width),
            buf(2, d_model, ff),
            pltpu.SemaphoreType.DMA((slots,)),
            pltpu.SemaphoreType.DMA((slots,)),
            pltpu.SemaphoreType.DMA((4 + 2 * n_ty,)),
            pltpu.SemaphoreType.DMA((12,)),
        ],
        compiler_params=pltpu.CompilerParams(collective_id=0, has_side_effects=True, vmem_limit_bytes=67_000_000),
        cost_estimate=pl.CostEstimate(flops=60_000_000_000, bytes_accessed=60_000_000, transcendentals=0),
        name="layer_front",
    )(split(x_act), split(cot_out), w_up, w_dt, w_a, vecs, b_qkv, b_up)


def tail_kernel(
    qkv, d_ctx, u, d_pre, h1, x, cot, w_d, w_a, w_u, vecs, small, cos_tab, sin_tab, turn_tab,
    y_out, dx_out, small_out, dw_out,
    qkv_b, dctx_b, u_b, dpre_b, h1_b, x_b, cot_b, q_s, k_s, dq_s, ctx_s, dqkv_s, acc, dbq, ln_acc, pw, dw_buf,
    part, rc, sy, ry, fin, x_own, c_own, sm_buf, send_sems, recv_sems, local_sems, *, n_tx, blk,
):
    g, z, t, core, y, t_core, t_y, t_diag = neighbours()
    core_dev, y_dev = (g, z, t_core), (g, z, t_y)
    z_dev = [(g, (z + k) % n_tx, t) for k in range(n_tx)]
    n_seq, seq, d_model = x.shape
    width = d_ctx.shape[-1]
    d_loc = d_model // n_tx
    heads, steps = width // HEAD, seq // blk
    sub = seq // 4
    links = Links(send_sems, recv_sems)
    outs = (y_out, dx_out)
    late = ((u, u_b), (d_pre, dpre_b), (h1, h1_b), (x, x_b), (cot, cot_b))

    def load_early(s):
        slot = s % 2
        return [
            pltpu.make_async_copy(qkv.at[s], qkv_b.at[slot], local_sems.at[slot]),
            pltpu.make_async_copy(d_ctx.at[s], dctx_b.at[slot], local_sems.at[2 + slot]),
        ]

    def load_late(s):
        return [pltpu.make_async_copy(src.at[s], dst, local_sems.at[4 + i]) for i, (src, dst) in enumerate(late)]

    for copy in load_early(0):
        copy.start()
    acc[...] = jnp.zeros_like(acc)
    dbq[...] = jnp.zeros_like(dbq)
    ln_acc[...] = jnp.zeros_like(ln_acc)
    enter([core_dev, y_dev] + z_dev[1:])

    def cols(s):
        return block(s, d_loc)

    def rows(c):
        return block(c, sub)

    core_slot = [[links.slot(n_seq) for _ in BOTH] for _ in BOTH]
    y_slot = [links.slot(n_seq) for _ in BOTH]
    z_slot = [[links.slot(n_seq) for _ in range(n_tx)] for _ in BOTH]
    ag_y = [[links.slot(n_seq) for _ in range(n_tx)] for _ in BOTH]
    ag_c = [[[links.slot(n_seq) for _ in BOTH] for _ in range(n_tx)] for _ in BOTH]
    sm_slot = [links.slot() for _ in range(5)]
    rs_slot = [links.slot() for _ in range(n_tx)]

    turn = turn_tab[...]

    def rotate(v, sign):
        return (v.astype(F32) * cos_tab[...] + sign * (dot_nn(v, turn) * sin_tab[...])).astype(BF16)

    def attend(s):
        slot = s % 2
        q_s[...] = rotate(qkv_b[slot, :, 0:width], 1.0) * BF16(HEAD ** -0.5)
        k_s[...] = rotate(qkv_b[slot, :, width:2 * width], 1.0)
        row = lax.broadcasted_iota(jnp.int32, (blk, blk), 0)
        col = lax.broadcasted_iota(jnp.int32, (blk, blk), 1)
        causal = row >= col
        dk_heads, dv_heads = [], []
        for h in range(heads):
            hs = slice(h * HEAD, (h + 1) * HEAD)
            k_h = k_s[:, hs]
            v_h = qkv_b[slot, :, 2 * width + h * HEAD:2 * width + (h + 1) * HEAD]
            dk = [None] * steps
            dv = [None] * steps
            for i in range(steps):
                at = slice(i * blk, (i + 1) * blk)
                n = (i + 1) * blk
                q_i = q_s[at, hs]
                do_i = dctx_b[slot, at, hs]
                sc = dot_nt(q_i, k_h[:n])
                s_diag = jnp.where(causal, sc[:, n - blk:], -1e30)
                sc = s_diag if i == 0 else jnp.concatenate([sc[:, :n - blk], s_diag], axis=1)
                p = jnp.exp(sc - jnp.max(sc, axis=1, keepdims=True))
                p = p * (1.0 / jnp.sum(p, axis=1, keepdims=True))
                p_b = p.astype(BF16)
                ctx_s[at, hs] = dot_nn(p_b, v_h[:n]).astype(BF16)
                dp = dot_nt(do_i, v_h[:n]).astype(BF16).astype(F32)
                ds = (p * (dp - jnp.sum(p * dp, axis=1, keepdims=True))).astype(BF16)
                dq_s[at, hs] = (dot_nn(ds, k_h[:n]) * HEAD ** -0.5).astype(BF16)
                dk_i = dot_tn(ds, q_i)
                dv_i = dot_tn(p_b, do_i)
                for j in range(i + 1):
                    part_k, part_v = dk_i[j * blk:(j + 1) * blk], dv_i[j * blk:(j + 1) * blk]
                    dk[j] = part_k if dk[j] is None else dk[j] + part_k
                    dv[j] = part_v if dv[j] is None else dv[j] + part_v
            dk_heads.append(jnp.concatenate(dk, axis=0).astype(BF16))
            dv_heads.append(jnp.concatenate(dv, axis=0).astype(BF16))
        pieces = (rotate(dq_s[...], -1.0), rotate(jnp.concatenate(dk_heads, axis=1), -1.0), jnp.concatenate(dv_heads, axis=1))
        for pos, piece in enumerate(pieces):
            at = slice(pos * width, (pos + 1) * width)
            dqkv_s[:, at] = piece
            dbq[:, at] += fold(piece.astype(F32))

    def forward_part(s):
        def body(r, carry):
            at = block(r, blk)
            total = dot_nt(u_b[at, :], w_d[...]) + dot_nt(ctx_s[at, :], w_a[:, 3 * width:])
            part[0, s, at, :] = total.astype(BF16)
            return carry
        lax.fori_loop(0, steps, body, 0)

    def backward_part(s):
        def body(r, carry):
            at = block(r, blk)
            d_h1 = dot_nt(dqkv_s[at, :], w_a[:, :3 * width]).astype(BF16).astype(F32)
            d_h2 = dot_nt(dpre_b[at, :], w_u[...]).astype(BF16).astype(F32)
            xf = x_b[at, :].astype(F32)
            xh, _ = normalise(xf)
            part[1, s, at, :] = (d_h1 * vecs[0:1, :] + d_h2 * vecs[1:2, :]).astype(BF16)
            for i, v in enumerate((d_h1 * xh, d_h1, d_h2 * xh, d_h2)):
                ln_acc[i] += fold(v)
            return carry
        lax.fori_loop(0, steps, body, 0)

    def weight_part():
        def body(r, carry):
            at = block(r, d_loc)
            acc[at, :3 * width] += dot_tn(h1_b[:, at], dqkv_s[...])
            acc[at, 3 * width:] += dot_tn(cot_b[:, at], ctx_s[...])
            return carry
        lax.fori_loop(0, n_tx, body, 0)

    def share(a, s):
        for j, yy in enumerate((1 - y, y)):
            links.send(core_slot[a][j] + s, part.at[a, s, rows(yy * 2 + 1 - core)], rc.at[a, s, yy], core_dev)

    step = 32

    def give(s):
        for a in BOTH:
            links.arrive(core_slot[a][0] + s, rc.at[a, s, 1 - y], core_dev)

            def body(r, carry):
                at = block(r, step)
                mine = part[a, s, pl.ds(pl.multiple_of(t_y * sub + r * step, step), step), :]
                sy[a, s, at, :] = (mine.astype(F32) + rc[a, s, 1 - y, at, :].astype(F32)).astype(BF16)
                return carry
            lax.fori_loop(0, sub // step, body, 0)
            links.send(y_slot[a] + s, sy.at[a, s], ry.at[a, s], y_dev)

    def finish(s):
        for a in BOTH:
            links.arrive(core_slot[a][1] + s, rc.at[a, s, y], core_dev)
            links.arrive(y_slot[a] + s, ry.at[a, s], y_dev)

            def body(r, carry):
                at = block(r, step)
                whole = pl.ds(pl.multiple_of(t * sub + r * step, step), step)
                total = part[a, s, whole, :].astype(F32) + rc[a, s, y, at, :].astype(F32) + ry[a, s, at, :].astype(F32)
                xf = x_own[s, at, :].astype(F32)
                if a == 0:
                    out = xf + total + vecs[2:3, :]
                else:
                    xh, inv = normalise(xf)
                    out = c_own[s, at, :].astype(F32) + inv * (total - row_mean(total) - xh * row_mean(total * xh))
                fin[a, s, at, :] = out.astype(BF16)
                return carry
            lax.fori_loop(0, sub // step, body, 0)
            place = outs[a].at[z * n_seq + s, rows(t)]
            for k in OTHERS:
                links.send(z_slot[a][k] + s, fin.at[a, s, :, cols((z + k) % n_tx)], place, z_dev[k])
            mine = fin.at[a, s, :, cols(z)]
            pltpu.make_async_copy(mine, place, local_sems.at[9 + a * n_seq + s]).start()
            links.send(ag_y[a][0] + s, mine, place, y_dev)
            links.send(ag_c[a][0][0] + s, mine, place, core_dev)

    def src(k):
        return (z + n_tx - k) % n_tx

    def forward(s):
        for a in BOTH:
            for k in OTHERS:
                place = outs[a].at[src(k) * n_seq + s, rows(t)]
                links.arrive(z_slot[a][k] + s, place, y_dev)
                links.send(ag_y[a][k] + s, place, place, y_dev)
                links.send(ag_c[a][k][0] + s, place, place, core_dev)

    def forward_y(s):
        for a in BOTH:
            for k in (0, *OTHERS):
                place = outs[a].at[src(k) * n_seq + s, rows(t_y)]
                links.arrive(ag_y[a][k] + s, place, y_dev)
                links.send(ag_c[a][k][1] + s, place, place, core_dev)

    def settle(s):
        for a in BOTH:
            for k in range(n_tx):
                for j, who in enumerate((t_core, t_diag)):
                    links.arrive(ag_c[a][k][j] + s, outs[a].at[src(k) * n_seq + s, rows(who)], core_dev)
            pltpu.make_async_copy(fin.at[a, s, :, cols(z)], outs[a].at[z * n_seq + s, rows(t)], local_sems.at[9 + a * n_seq + s]).wait()
        done(s)

    def done(s):
        for a in BOTH:
            for j, yy in enumerate((1 - y, y)):
                links.make(core_slot[a][j] + s, part.at[a, s, rows(yy * 2 + 1 - core)], rc.at[a, s, yy], core_dev).wait_send()
            links.make(y_slot[a] + s, sy.at[a, s], ry.at[a, s], y_dev).wait_send()
            for k in range(n_tx):
                mine = fin.at[a, s, :, cols((z + k) % n_tx)]
                place = outs[a].at[src(k) * n_seq + s, rows(t)]
                if k:
                    links.make(z_slot[a][k] + s, mine, place, z_dev[k]).wait_send()
                links.make(ag_y[a][k] + s, place, place, y_dev).wait_send()
                for j in BOTH:
                    links.make(ag_c[a][k][j] + s, place, place, core_dev).wait_send()

    own_in = [
        pltpu.make_async_copy(x.at[:, rows(t), :], x_own, local_sems.at[9 + 2 * n_seq]),
        pltpu.make_async_copy(cot.at[:, rows(t), :], c_own, local_sems.at[10 + 2 * n_seq]),
    ]
    for copy in own_in:
        copy.start()
    for copy in own_in:
        copy.wait()

    def one(s, carry):
        for copy in load_early(s):
            copy.wait()

        @pl.when(s < n_seq - 1)
        def _():
            for copy in load_early(s + 1):
                copy.start()

        for copy in load_late(s):
            copy.start()
        attend(s)
        for copy in load_late(s):
            copy.wait()
        forward_part(s)
        share(0, s)
        backward_part(s)
        share(1, s)
        weight_part()
        give(s)

        @pl.when(s > 0)
        def _():
            finish(s - 1)

        return carry

    lax.fori_loop(0, n_seq, one, 0)
    last = n_seq - 1
    pw[...] = acc[...].astype(BF16)
    for k in OTHERS:
        links.send(rs_slot[k], pw.at[cols((z + k) % n_tx)], dw_buf.at[k - 1], z_dev[k])
    for i in range(4):
        sm_buf[0, i:i + 1, :] = ln_acc[i].sum(0, keepdims=True)
    sm_buf[0, 4:5, :] = small[4:5, :]
    sm_buf[0, 5:6, 0:3 * width] = dbq[...].sum(0, keepdims=True)
    sm_buf[0, 5:6, 3 * width:] = jnp.zeros((1, d_model - 3 * width), F32)
    sm_buf[0, 6:8, :] = jnp.zeros((2, d_model), F32)
    links.send(sm_slot[0], sm_buf.at[0], sm_buf.at[1], core_dev)
    row = lax.broadcasted_iota(jnp.int32, (8, d_model), 0)
    forward(0)
    finish(last)
    links.arrive(sm_slot[0], sm_buf.at[1], core_dev)
    sm_buf[2] = sm_buf[0] + jnp.where(row < 4, sm_buf[1], 0.0)
    links.send(sm_slot[1], sm_buf.at[2], sm_buf.at[3], y_dev)
    forward(1)
    forward_y(0)
    links.arrive(sm_slot[1], sm_buf.at[3], y_dev)
    sm_buf[4] = sm_buf[2] + jnp.where(row < 4, sm_buf[3], 0.0)
    for k in OTHERS:
        links.send(sm_slot[1 + k], sm_buf.at[4], sm_buf.at[4 + k], z_dev[k])
    forward(last)
    forward_y(1)
    forward_y(last)
    for k in OTHERS:
        links.arrive(rs_slot[k], dw_buf.at[k - 1], y_dev)
    dw_out[...] = acc[cols(z), :]
    for k in OTHERS:
        dw_out[...] += dw_buf[k - 1].astype(F32)
    for k in OTHERS:
        links.arrive(sm_slot[1 + k], sm_buf.at[4 + k], y_dev)
    small_out[...] = sm_buf[4] + sm_buf[5] + sm_buf[6] + sm_buf[7]
    for s in range(n_seq):
        settle(s)
    for k in OTHERS:
        links.make(rs_slot[k], pw.at[cols((z + k) % n_tx)], dw_buf.at[k - 1], z_dev[k]).wait_send()
        links.make(sm_slot[1 + k], sm_buf.at[4], sm_buf.at[4 + k], z_dev[k]).wait_send()
    links.make(sm_slot[0], sm_buf.at[0], sm_buf.at[1], core_dev).wait_send()
    links.make(sm_slot[1], sm_buf.at[2], sm_buf.at[3], y_dev).wait_send()


def layer_tail(qkv, d_ctx, u, d_pre, h1, x, cot, w_d, w_a, w_u, vecs, small, n_tx, n_ty):
    n_seq, seq, d_model = x.shape
    width, d_loc, blk, sub = d_ctx.shape[-1], d_model // n_tx, 256, seq // n_ty
    any_spec, vmem = pl.BlockSpec(memory_space=pl.ANY), pl.BlockSpec(memory_space=pltpu.VMEM)
    out = jax.ShapeDtypeStruct((n_seq * n_tx, seq, d_loc), BF16)
    cos_tab, sin_tab = rope_tables(seq, width)
    slots = n_seq * 2 * (3 + 4 * n_tx) + 5 + n_tx
    wide = lambda *lead: pltpu.VMEM(lead + (seq, d_model), BF16)
    piece = lambda *lead: pltpu.VMEM(lead + (sub, d_model), BF16)
    return pl.pallas_call(
        functools.partial(tail_kernel, n_tx=n_tx, blk=blk),
        in_specs=[any_spec] * 7 + [vmem] * 8,
        out_specs=[any_spec, any_spec, vmem, vmem],
        out_shape=[out, out, jax.ShapeDtypeStruct((8, d_model), F32), jax.ShapeDtypeStruct((d_loc, d_model), F32)],
        scratch_shapes=[
            pltpu.VMEM((2, seq, 3 * width), BF16),
            pltpu.VMEM((2, seq, width), BF16),
            wide(), wide(), wide(), wide(), wide(),
            pltpu.VMEM((seq, width), BF16),
            pltpu.VMEM((seq, width), BF16),
            pltpu.VMEM((seq, width), BF16),
            pltpu.VMEM((seq, width), BF16),
            pltpu.VMEM((seq, 3 * width), BF16),
            pltpu.VMEM((d_model, d_model), F32),
            pltpu.VMEM((8, 3 * width), F32),
            pltpu.VMEM((4, 8, d_model), F32),
            pltpu.VMEM((d_model, d_model), BF16),
            pltpu.VMEM((n_tx - 1, d_loc, d_model), BF16),
            wide(2, n_seq),
            piece(2, n_seq, 2),
            piece(2, n_seq),
            piece(2, n_seq),
            piece(2, n_seq),
            piece(n_seq),
            piece(n_seq),
            pltpu.VMEM((8, 8, d_model), F32),
            pltpu.SemaphoreType.DMA((slots,)),
            pltpu.SemaphoreType.DMA((slots,)),
            pltpu.SemaphoreType.DMA((11 + 2 * n_seq,)),
        ],
        compiler_params=pltpu.CompilerParams(collective_id=1, has_side_effects=True, vmem_limit_bytes=67_000_000),
        cost_estimate=pl.CostEstimate(flops=60_000_000_000, bytes_accessed=60_000_000, transcendentals=0),
        name="layer_tail",
    )(qkv, d_ctx, u, d_pre, h1, x, cot, w_d, w_a, w_u, vecs, small, cos_tab, sin_tab, rope_turn(width))


def solution(mesh):
    n_tx, n_ty = mesh.shape['tx'], mesh.shape['ty']
    act_spec = P('dp', None, 'tx')
    width_spec = P('tx')
    in_specs = (act_spec, act_spec, width_spec, width_spec, width_spec, width_spec, P('tx', 'ty', None), P('ty', None), P('ty', 'tx'), width_spec, P('tx', 'ty'), P('ty'), P('ty', 'tx'), width_spec)
    width_out = P(('dp', 'tx'))
    out_specs = (act_spec, act_spec, width_out, width_out, width_out, width_out, P(('dp', 'tx'), 'ty', None), P(('dp', 'ty'), None), P(('dp', 'ty'), 'tx'), width_out, P(('dp', 'tx'), 'ty'), P(('dp', 'ty')), P(('dp', 'ty'), 'tx'), width_out)
    def body(x_act, cot_out, ln1_gain, ln1_bias, ln2_gain, ln2_bias, w_qkv, b_qkv, w_dense, b_dense, w_up, b_up, w_down, b_down):
        batch, seq, d_loc = x_act.shape
        d_model = d_loc * n_tx
        heads = w_qkv.shape[1]
        hw = heads * HEAD
        n_b = batch // n_tx
        tok = n_b * seq
        z, g = lax.axis_index('tx'), lax.axis_index('dp')

        wq_loc = w_qkv.reshape(d_loc, heads, 3, HEAD).transpose(0, 2, 1, 3).reshape(d_loc, 3 * hw)
        vec_loc = jnp.stack([ln1_gain, ln1_bias, ln2_gain, ln2_bias, b_dense, b_down], axis=0)
        vec_loc = jnp.pad(vec_loc, ((0, 10), (0, 0)))
        bq = b_qkv.astype(F32).reshape(heads, 3, HEAD).transpose(1, 0, 2).reshape(1, 3 * hw)
        row8 = lambda a: jnp.pad(a, ((0, 7), (0, 0)))
        x, cot, w_u, w_dt, w_a, vecs, h1, qkv, u, d_pre, d_ctx, part_down, part_up, d_bup = layer_front(
            x_act, cot_out, w_up, w_down.T, jnp.concatenate([wq_loc, w_dense.T], axis=1), vec_loc, row8(bq), row8(b_up.astype(F32)[None]), n_tx, n_ty)
        g1, g2, b_o, b_d = [vecs[i].astype(F32) for i in (0, 2, 4, 5)]

        def scatter_grad(part):
            return lax.psum_scatter(part, 'tx', scatter_dimension=0, tiled=True)

        sum_down, sum_up = scatter_grad(part_down), scatter_grad(part_up)
        d_w_down, d_w_up = sum_down.astype(F32).T, sum_up.astype(F32)
        d_b_up = d_bup.sum(0)
        small = jnp.pad(d_b_up[None], ((4, 3), (0, d_model - d_b_up.shape[0])))
        rows = jnp.pad(jnp.stack([g1, g2, b_o + b_d], axis=0), ((0, 5), (0, 0)))
        by_seq = lambda a: a.reshape(n_b, seq, a.shape[-1])
        y_out, dx_act, total, d_w_a = layer_tail(by_seq(qkv), by_seq(d_ctx), by_seq(u), by_seq(d_pre), by_seq(h1), by_seq(x), by_seq(cot), w_dt, w_a, w_u, rows, small, n_tx, n_ty)
        d_w_qkv = d_w_a[:, :3 * hw].reshape(d_loc, 3, heads, HEAD).transpose(0, 2, 1, 3).reshape(d_loc, heads, 3 * HEAD)
        d_w_dense = d_w_a[:, 3 * hw:].T
        ln_sum = lax.dynamic_slice(total, (0, z * d_loc), (4, d_loc))
        d_b_up = total[4, :d_b_up.shape[0]]
        d_b_qkv = total[5, :3 * hw].reshape(3, heads, HEAD).transpose(1, 0, 2).reshape(heads, 3 * HEAD)
        d_b_out = cot_out.astype(F32).sum((0, 1))
        return (y_out, dx_act, ln_sum[0], ln_sum[1], ln_sum[2], ln_sum[3], d_w_qkv, d_b_qkv, d_w_dense, d_b_out, d_w_up, d_b_up, d_w_down, d_b_out)

    return jax.shard_map(body, mesh=mesh, in_specs=in_specs, out_specs=out_specs, check_vma=False)
```

profile of v0, /device:TPU:0, one launch (start us, length us, event | category | flops | bytes accessed | tf_op | source)
XLA Modules:
  0.0 374.0 jit_solution(17901816468998487904)
XLA Ops:
  7.2 0.0 reduce-scatter.5.cloned.1.call-start
  7.2 0.7 stack.27
  7.9 0.7 stack.28
  8.5 0.7 stack.29
  9.2 0.7 stack.30
  9.9 0.7 stack.31
  10.5 0.7 stack.32
  11.2 0.8 reshape.97
  11.9 0.1 reshape.98
  12.0 0.7 broadcast_in_dim.9
  12.7 0.6 pad_convert_fusion.1.b_qkv
  13.3 0.6 pad_convert_fusion.b_up
  14.0 1.0 copy.48
  15.0 1.0 copy.47
  16.0 0.2 copy.49
  16.2 2.0 copy.46
  18.2 0.6 pad.32.v_in
  18.8 0.9 pad_maximum_fusion.wa_in
  19.7 132.2 %layer_front.1 = (bf16[2304,1024]{1,0:T(8,128)(2,1)}, bf16[2304,1024]{1,0:T(8,128)(2,1)}, bf16[1024,1024]{1,0:T(8,128)(2,1)}, bf16[1024,1024]{1,0:T(8,128)(2,1)}...) custom-call(bf16[4,4,576,256]{3,2,1,0:T(8,128)(2,1)} %bitcast.54, ...), custom_call_target="tpu_custom_call" | custom-call | flops 60000002048 | bytes 60000000 | tf_op jit(solution)/shard_map/layer_front/pallas_call | solution.py:325
  151.9 0.0 copy-start.1
  151.9 0.0 reduce-scatter.5.cloned.1.call-update
  152.0 0.0 reduce-scatter.3.cloned.1.call-start
  152.0 0.7 reduce-scatter.3.cloned.1.call-update
  152.8 0.0 copy-start
  152.8 3.6 convert_reduce_fusion
  156.3 0.0 copy-start.2
  156.4 0.0 copy-done.1
  156.4 0.1 iota_multiply_fusion
  156.5 0.1 fusion.3
  156.6 0.1 tile.8
  156.7 1.1 copy.51.cos_tab
  157.8 0.1 tile.20
  157.9 1.1 copy.52.sin_tab
  159.0 0.0 copy-done
  159.1 0.6 pad.38.small
  159.7 0.6 select_maximum_fusion.vecs
  160.3 0.7 subtract_convert_fusion.turn_tab
  161.0 185.1 %layer_tail.1 = (bf16[12,768,256]{2,1,0:T(8,128)(2,1)}, bf16[12,768,256]{2,1,0:T(8,128)(2,1)}, f32[8,1024]{1,0:T(8,128)}, f32[256,1024]{1,0:T(8,128)}) custom-call(bf16[3,768,768]{2,1,0:T(8,128)(2,1)} %bitcast.60, bf16[3,768,256]{2,1,0:T(8,128)(2,1)} %bitcast.61, bf16[3,768,1024]{2,1,0:T(8,128)(2,1)} %bitcast.58, bf16[3,768,1024]{2,1,0:T(8,128)(2,1)} %bitcast.59, ...), custom_call_target="tpu_custom_call" | custom-call | flops 60000002048 | bytes 60000000 | tf_op jit(solution)/shard_map/layer_tail/pallas_call | solution.py:648
  346.2 1.4 slice.47
  347.6 0.8 slice_reduce_fusion
  348.3 0.1 reshape_squeeze.3
  348.4 0.7 reshape.108
  349.1 1.2 slice.44
  350.3 0.3 copy.53
  350.5 1.0 copy.54
  351.5 1.0 slice_bitcast_fusion
  352.5 0.8 copy.56
  353.3 1.5 fusion.6
  354.8 0.0 reduce-scatter.5.cloned.1.call-done
  354.8 1.1 convert_bitcast_fusion
  355.9 1.3 copy.57
  357.3 0.0 reduce-scatter.3.cloned.1.call-done
  357.3 0.0 slice-start
  357.3 2.3 convert_element_type.54
  359.5 0.0 copy-done.2
  359.5 0.6 copy.63
  360.1 0.0 slice-start.1
  360.1 4.9 %copy.64 = bf16[12,768,256]{2,1,0:T(8,128)(2,1)} copy(bf16[12,768,256]{2,1,0:T(8,128)(2,1)} %get-tuple-element.146) | data formatting | bytes 9437184
  365.0 0.0 slice-done
  365.0 0.0 slice-done.1
  365.0 2.2 copy.65
  (13 shorter events, 0.1 us)
Async XLA Ops:
  7.2 347.6 %reduce-scatter.5.cloned.1.call-start = ((), (), s32[]{:S(2)}) async-start(), calls=%async_computation.3 | async-start | bytes 2621440 | tf_op jit(solution)/shard_map/reduce_scatter | solution.py:711
  151.9 4.4 %copy-start.1 = (bf16[16,1024]{1,0:T(8,128)(2,1)S(1)}, bf16[16,1024]{1,0:T(8,128)(2,1)}, u32[]{:S(2)}) copy-start(bf16[16,1024]{1,0:T(8,128)(2,1)} %get-tuple-element.42) | copy-start | bytes 98308
  152.0 205.3 %reduce-scatter.3.cloned.1.call-start = ((), (), s32[]{:S(2)}) async-start(), calls=%async_computation.2 | async-start | bytes 2621440 | tf_op jit(solution)/shard_map/reduce_scatter | solution.py:711
  152.8 6.3 %copy-start = (f32[8,1024]{1,0:T(8,128)S(1)}, f32[8,1024]{1,0:T(8,128)}, u32[]{:S(2)}) copy-start(f32[8,1024]{1,0:T(8,128)} %get-tuple-element.43) | copy-start | bytes 98308
  156.3 203.2 %copy-start.2 = (f32[256]{0:T(256)}, f32[256]{0:T(256)S(1)}, u32[]{:S(2)}) copy-start(f32[256]{0:T(256)S(1)} %convert_reduce_fusion) | copy-start | bytes 3076
  357.3 7.7 %slice-start = ((s8[4718592]{0:T(1024)(128)(4,1)}), s8[4194304]{0:T(1024)(128)(4,1)S(1)}, s32[]{:S(2)}) async-start(s8[4718592]{0:T(1024)(128)(4,1)} %bitcast.36), calls=%async_computation.4 | async-start | bytes 8388608
  360.1 4.9 %slice-start.1 = ((s8[4718592]{0:T(1024)(128)(4,1)}), s8[524288]{0:T(1024)(128)(4,1)S(1)}, s32[]{:S(2)}) async-start(s8[4718592]{0:T(1024)(128)(4,1)} %bitcast.36), calls=%async_computation.5 | async-start | bytes 1048576
Sparse Core Ops, SparseCore 0:
  152.1 42.6 reduce-scatter.4
  197.0 61.0 reduce-scatter.2
where the time goes:
time: 375 us; the launch traced here: 374 us
  Pallas kernels  317 us (85%)
  local copies, waits for them, and re-layouts  31 us (8%)
  between operations  14.2 us (4%)
  other arithmetic  10.7 us (3%)
    pallas_call x1, Pallas kernels, layer_tail(): pl.pallas_call(functools.partial(tail_kernel, n_tx=n_tx, blk=blk), in_spe...  185 us
    pallas_call x1, Pallas kernels, layer_front(): pl.pallas_call(functools.partial(front_kernel, n_tx=n_tx, n_ty=n_ty, blk=...  132 us
    unnamed x17, local copies, waits for them, and re-layouts  12.8 us
  transfers between devices with their start and end apart: 2, of which 0 were waited for; matrix products, arithmetic and copies ran while one was open for 5% of the time, Pallas kernels for 50%

commit v1 on v0

--- a/solution.py
+++ b/solution.py
@@ -63,6 +63,14 @@
     return (v - mean) * inv_std, inv_std
 
 
+def row_sum(v):
+    return jnp.sum(v, axis=-1, keepdims=True)
+
+
+def loop(count, body):
+    lax.fori_loop(0, count, lambda i, carry: (body(i), carry)[1], 0)
+
+
 def fold(v):
     return v.reshape(v.shape[0] // 8, 8, v.shape[1]).sum(0)
 
@@ -111,13 +119,14 @@
 def front_kernel(
     x_in, c_in, wu_in, wd_in, wa_in, v_in, b_qkv, b_up,
     x_out, c_out, wu_out, wd_out, wa_out, v_out, h1_out, qkv_out, u_out, dpre_out, dctx_out, dwd_out, dwu_out, dbup_out,
-    x_v, c_v, wu_v, wd_v, wa_v, h1_v, h2_v, u_v, gp_v, qkv_v, dpre_v, dctx_v, dw_v,
+    x_v, c_v, wu_v, wd_v, wa_v, h1_v, h2_v, u_v, gp_v, qkv_v, dpre_v, dctx_v, dwd_v, dwu_v,
     send_sems, recv_sems, local_sems, out_sems, *, n_tx, n_ty, blk,
 ):
     g, z, t, core, y, t_core, t_y, t_diag = neighbours()
     core_dev, y_dev, x_dev = (g, z, t_core), (g, z, t_y), (1 - g, z, t)
     z_dev = [(g, (z + k) % n_tx, t) for k in range(n_tx)]
     left, right = (g, z - 1, t), (g, z + 1, t)
+    end = n_tx - 1
     d_loc = x_in.shape[-1]
     half = d_loc // 2
     tok = x_v.shape[0]
@@ -150,7 +159,7 @@
 
     def w_send(w, hops, src):
         s_left, s_right = z - hops, z + hops
-        links.send(w_slot[w][hops + 1], src(s_left), weights[w][1].at[w_rows(s_left, g), :], right, (s_left >= 0) & (z < n_tx - 1))
+        links.send(w_slot[w][hops + 1], src(s_left), weights[w][1].at[w_rows(s_left, g), :], right, (s_left >= 0) & (z < end))
         links.send(w_slot[w][n_tx + hops + 1], src(s_right), weights[w][1].at[w_rows(s_right, g), :], left, (s_right < n_tx) & (z > 0))
 
     def w_start(w):
@@ -166,7 +175,7 @@
             place = out.at[w_rows(s, g), :]
             links.arrive(w_slot[w][slot], place, right, ok)
             links.send(x_slot[w][x_at], place, place, x_dev, ok)
-        if hops < n_tx - 1:
+        if hops < end:
             w_send(w, hops, lambda s: out.at[w_rows(s, g), :])
 
     def w_finish(w):
@@ -203,25 +212,24 @@
             for j, c in enumerate((t_core, t_diag)):
                 links.arrive(c_slot[a][k][j], arrays[a][1].at[rows(c), src_cols(k)], core_dev)
 
-    w_start(0)
-    w_start(1)
+    for w in BOTH:
+        w_start(w)
     for k in OTHERS:
         links.send(v_slot[k], v_in, v_out.at[:, cols(z)], z_dev[k])
     t_start(0)
-    w_pass(0, 1)
-    w_pass(1, 1)
+    for w in BOTH:
+        w_pass(w, 1)
     for k in OTHERS:
         t_pass(0, k)
-    w_pass(0, 2)
-    w_pass(1, 2)
+    for w in BOTH:
+        w_pass(w, 2)
     w_start(2)
     t_start(1)
     for k in OTHERS:
         t_pass_y(0, k)
-    w_pass(0, 3)
-    w_pass(1, 3)
-    w_finish(0)
-    w_finish(1)
+    for w in BOTH:
+        w_pass(w, 3)
+        w_finish(w)
     t_finish(0)
     for k in OTHERS:
         links.arrive(v_slot[k], v_out.at[:, src_cols(k)], y_dev)
@@ -238,33 +246,33 @@
     write(x_v, x_out)
     write(wu_v, wu_out)
     write(wa_v, wa_out)
-    late_steps = {
-        0: lambda: w_pass(2, 1),
-        2: lambda: [t_pass(1, k) for k in OTHERS],
-        3: lambda: w_pass(2, 2),
-        4: lambda: [t_pass_y(1, k) for k in OTHERS],
-        6: lambda: w_pass(2, 3),
-    }
+
+    def tokens(step):
+        for k in OTHERS:
+            step(1, k)
+
+    late_steps = tuple(enumerate((lambda: w_pass(2, 1), None, lambda: tokens(t_pass), lambda: w_pass(2, 2), lambda: tokens(t_pass_y), None, lambda: w_pass(2, 3))))
     vec = v_out[...].astype(F32)
-
-    def forward(i, carry):
+    g1, be1, g2, be2 = [vec[i:i + 1] for i in range(4)]
+
+    def forward(i):
         at = block(i, blk)
         xf = x_v[at, :].astype(F32)
         xh, _ = normalise(xf)
-        h1 = (xh * vec[0:1] + vec[1:2]).astype(BF16)
-        h2 = (xh * vec[2:3] + vec[3:4]).astype(BF16)
+        h1 = (xh * g1 + be1).astype(BF16)
+        h2 = (xh * g2 + be2).astype(BF16)
         h1_v[at, :] = h1
         h2_v[at, :] = h2
-        qkv_v[at, :] = (dot_nn(h1, wa_v[:, :3 * width]) + b_qkv[0:1, :]).astype(BF16)
-        pre = (dot_nn(h2, wu_v[...]) + b_up[0:1, :]).astype(BF16).astype(F32)
+        qkv_v[at, :] = (dot_nn(h1, wa_v[:, :3 * width]) + b_qkv[...]).astype(BF16)
+        pre = (dot_nn(h2, wu_v[...]) + b_up[...]).astype(BF16).astype(F32)
         cdf = 0.5 * (1.0 + lax.erf(pre * (0.5 ** 0.5)))
         u_v[at, :] = (pre * cdf).astype(BF16)
         gp_v[at, :] = cdf + pre * (jnp.exp(-0.5 * pre * pre) * (1.0 / (2.0 * jnp.pi) ** 0.5))
-        for when, what in late_steps.items():
-            pl.when(i == when)(lambda: (what(), None)[1])
-        return carry
-
-    lax.fori_loop(0, tok // blk, forward, 0)
+        for when, what in late_steps:
+            if what:
+                pl.when(i == when)(what)
+
+    loop(tok // blk, forward)
     write(h1_v, h1_out)
     write(qkv_v, qkv_out)
     write(u_v, u_out)
@@ -274,7 +282,7 @@
     write(wd_v, wd_out)
     dbup_out[...] = jnp.zeros_like(dbup_out)
 
-    def backward(i, carry):
+    def backward(i):
         at = block(i, blk)
         cot = c_v[at, :]
         d_gelu = dot_nn(cot, wd_v[...]).astype(BF16).astype(F32)
@@ -282,17 +290,21 @@
         dpre_v[at, :] = d_pre
         dbup_out[...] += fold(d_pre.astype(F32))
         dctx_v[at, :] = dot_nn(cot, wa_v[:, 3 * width:]).astype(BF16)
-        return carry
-
-    lax.fori_loop(0, tok // blk, backward, 0)
+
+    loop(tok // blk, backward)
     write(dpre_v, dpre_out)
     write(dctx_v, dctx_out)
-    for i, (lhs, rhs, out) in enumerate(((c_v, u_v, dwd_out), (h2_v, dpre_v, dwu_out))):
-        def weight(r, carry):
-            dw_v[i, cols(r), :] = dot_tn(lhs[:, cols(r)], rhs[...]).astype(BF16)
-            return carry
-        lax.fori_loop(0, n_tx, weight, 0)
-        write(dw_v.at[i], out)
+
+    def down(r):
+        dwd_v[r] = dot_tn(u_v[...], c_v[:, cols(r)]).astype(BF16)
+
+    def up(r):
+        dwu_v[r] = dot_tn(h2_v[:, cols(r)], dpre_v[...]).astype(BF16)
+
+    loop(n_tx, down)
+    write(dwd_v, dwd_out)
+    loop(n_tx, up)
+    write(dwu_v, dwu_out)
     piece = x_v.at[pl.ds(0, chunk), pl.ds(0, d_loc)]
     for a in BOTH:
         for k in OTHERS:
@@ -304,8 +316,8 @@
             if hops:
                 for _, x_at, _, ok in w_sides(hops):
                     links.sent(x_slot[w][x_at], shard, ok)
-            if hops < n_tx - 1:
-                links.sent(w_slot[w][hops + 1], shard, (z - hops >= 0) & (z < n_tx - 1))
+            if hops < end:
+                links.sent(w_slot[w][hops + 1], shard, (z - hops >= 0) & (z < end))
                 links.sent(w_slot[w][n_tx + hops + 1], shard, (z + hops < n_tx) & (z > 0))
     for k in OTHERS:
         links.sent(v_slot[k], v_in)
@@ -328,13 +340,14 @@
         out_specs=[any_spec] * 5 + [vmem] + [any_spec] * 7 + [vmem],
         out_shape=[
             arr(tok, d_model), arr(tok, d_model), arr(d_model, ff), arr(d_model, ff), arr(d_model, 4 * width), arr(vecs.shape[0], d_model),
-            arr(tok, d_model), arr(tok, 3 * width), arr(tok, ff), arr(tok, ff), arr(tok, width), arr(d_model, ff), arr(d_model, ff),
+            arr(tok, d_model), arr(tok, 3 * width), arr(tok, ff), arr(tok, ff), arr(tok, width), arr(n_tx, ff, d_loc), arr(n_tx, d_loc, ff),
             jax.ShapeDtypeStruct((8, ff), F32),
         ],
         scratch_shapes=[
             buf(tok, d_model), buf(tok, d_model), buf(d_model, ff), buf(d_model, ff), buf(d_model, 4 * width),
             buf(tok, d_model), buf(tok, d_model), buf(tok, ff), pltpu.VMEM((tok, ff), F32), buf(tok, 3 * width), buf(tok, ff), buf(tok, width),
-            buf(2, d_model, ff),
+            buf(n_tx, ff, d_loc),
+            buf(n_tx, d_loc, ff),
             pltpu.SemaphoreType.DMA((slots,)),
             pltpu.SemaphoreType.DMA((slots,)),
             pltpu.SemaphoreType.DMA((4 + 2 * n_ty,)),
@@ -347,15 +360,16 @@
 
 
 def tail_kernel(
-    qkv, d_ctx, u, d_pre, h1, x, cot, w_d, w_a, w_u, vecs, small, cos_tab, sin_tab, turn_tab,
-    y_out, dx_out, small_out, dw_out,
-    qkv_b, dctx_b, u_b, dpre_b, h1_b, x_b, cot_b, q_s, k_s, dq_s, ctx_s, dqkv_s, acc, dbq, ln_acc, pw, dw_buf,
-    part, rc, sy, ry, fin, x_own, c_own, sm_buf, send_sems, recv_sems, local_sems, *, n_tx, blk,
+    qkv, d_ctx, u, d_pre, h1, x, cot, w_d, w_a, w_u, p_down, p_up, vecs, small, cos_tab, sin_tab, turn_tab,
+    y_out, dx_out, small_out, d_down, d_up, d_a,
+    qkv_b, dctx_b, u_b, dpre_b, h1_b, x_b, cot_b, q_s, k_s, dq_s, ctx_s, dqkv_s, acc, dbq, ln_acc, arr_down, arr_up, arr_a, own_down, own_up,
+    part, rc, sy, ry, x_own, c_own, sm_buf, send_sems, recv_sems, local_sems, rs_sems, *, n_tx, blk,
 ):
     g, z, t, core, y, t_core, t_y, t_diag = neighbours()
     core_dev, y_dev = (g, z, t_core), (g, z, t_y)
     z_dev = [(g, (z + k) % n_tx, t) for k in range(n_tx)]
     n_seq, seq, d_model = x.shape
+    end = n_tx - 1
     width = d_ctx.shape[-1]
     d_loc = d_model // n_tx
     heads, steps = width // HEAD, seq // blk
@@ -392,9 +406,84 @@
     z_slot = [[links.slot(n_seq) for _ in range(n_tx)] for _ in BOTH]
     ag_y = [[links.slot(n_seq) for _ in range(n_tx)] for _ in BOTH]
     ag_c = [[[links.slot(n_seq) for _ in BOTH] for _ in range(n_tx)] for _ in BOTH]
-    sm_slot = [links.slot() for _ in range(5)]
-    rs_slot = [links.slot() for _ in range(n_tx)]
-
+    sm_slot = [links.slot() for _ in range(8)]
+
+    arrivals, owners, results = (arr_down, arr_up, arr_a), ((p_down, own_down), (p_up, own_up)), (d_down, d_up, d_a)
+    rs_slot = [[links.slot() for _ in range(5)] for _ in arrivals]
+    right, left = (g, z + 1, t), (g, z - 1, t)
+    first, last_z = z == 0, z == end
+    middle = (z > 0) & (z < end)
+    lower = z < n_tx // 2
+    R0, L0, R1, L1, FAR = range(5)
+
+    def rs_load(w, slot, d):
+        return pltpu.make_async_copy(owners[w][0].at[d], owners[w][1].at[slot], rs_sems.at[w, slot])
+
+    def rs_send(w, name, dev, cond, src=None):
+        place = arrivals[w].at[name]
+        links.send(rs_slot[w][name], place if src is None else src, place, dev, cond)
+
+    def rs_add(w, name, slot, d, move_from, cond):
+        place = arrivals[w].at[move_from]
+
+        @pl.when(cond)
+        def _():
+            links.arrive(rs_slot[w][move_from], place, right)
+            size = place.shape[0] // 4
+
+            def body(r):
+                at = block(r, size)
+                mine = acc[pl.ds(pl.multiple_of(d * d_loc + r * size, size), size), :] if w >= len(owners) else owners[w][1][slot, at, :].astype(F32)
+                arrivals[w][move_from, at, :] = (arrivals[w][move_from, at, :].astype(F32) + mine).astype(BF16)
+            loop(4, body)
+
+    def rs_start(w):
+        for way, near, cond, to in ((1, (R0, R1, FAR), first, right), (-1, (L0, L1, FAR), last_z, left)):
+            for hop in (2, 1, 0):
+                d, name = z + way * (hop + 1), near[hop]
+                if w >= len(owners):
+                    @pl.when(cond)
+                    def _():
+                        arrivals[w][name] = acc[cols(d), :].astype(BF16)
+                    rs_send(w, name, to, cond)
+                else:
+                    rs_send(w, name, to, cond, owners[w][0].at[d])
+
+    def rs_far(w):
+        if w < len(owners):
+            rs_load(w, 0, 0).wait()
+        rs_add(w, R1, 0, (end) * (2 - z), FAR, middle)
+        links.send(rs_slot[w][R1], arrivals[w].at[FAR], arrivals[w].at[R1], right, middle & lower)
+        links.send(rs_slot[w][L1], arrivals[w].at[FAR], arrivals[w].at[L1], left, middle & (~lower))
+        if w < len(owners):
+            rs_load(w, 0, (z + end) % n_tx).start()
+
+    def rs_near(w):
+        for slot, name, source, to, d in ((1, R0, R1, right, z + 1), (0, L0, L1, left, z - 1)):
+            if w < len(owners):
+                rs_load(w, slot, 0).wait()
+            rs_add(w, name, slot, d, source, middle)
+            links.send(rs_slot[w][name], arrivals[w].at[source], arrivals[w].at[name], to, middle)
+            if w < len(owners) and slot:
+                rs_load(w, slot, z).start()
+
+    def rs_end(w):
+        if w < len(owners):
+            rs_load(w, 1, 0).wait()
+            results[w][...] = owners[w][1][1].astype(F32)
+        else:
+            results[w][...] = acc[cols(z), :]
+        for name, cond in ((R0, z > 0), (L0, z < end)):
+            @pl.when(cond)
+            def _():
+                links.arrive(rs_slot[w][name], arrivals[w].at[name], right)
+                results[w][...] += arrivals[w][name].astype(F32)
+
+    for w in BOTH:
+        rs_load(w, 0, (end) * (1 - z // 2)).start()
+        rs_load(w, 1, (z + 1) % n_tx).start()
+
+    gain1, gain2, bias = [vecs[i:i + 1, :] for i in range(3)]
     turn = turn_tab[...]
 
     def rotate(v, sign):
@@ -422,12 +511,12 @@
                 sc = dot_nt(q_i, k_h[:n])
                 s_diag = jnp.where(causal, sc[:, n - blk:], -1e30)
                 sc = s_diag if i == 0 else jnp.concatenate([sc[:, :n - blk], s_diag], axis=1)
-                p = jnp.exp(sc - jnp.max(sc, axis=1, keepdims=True))
-                p = p * (1.0 / jnp.sum(p, axis=1, keepdims=True))
+                p = jnp.exp(sc - jnp.max(sc, axis=-1, keepdims=True))
+                p = p * (1.0 / row_sum(p))
                 p_b = p.astype(BF16)
                 ctx_s[at, hs] = dot_nn(p_b, v_h[:n]).astype(BF16)
                 dp = dot_nt(do_i, v_h[:n]).astype(BF16).astype(F32)
-                ds = (p * (dp - jnp.sum(p * dp, axis=1, keepdims=True))).astype(BF16)
+                ds = (p * (dp - row_sum(p * dp))).astype(BF16)
                 dq_s[at, hs] = (dot_nn(ds, k_h[:n]) * HEAD ** -0.5).astype(BF16)
                 dk_i = dot_tn(ds, q_i)
                 dv_i = dot_tn(p_b, do_i)
@@ -444,37 +533,34 @@
             dbq[:, at] += fold(piece.astype(F32))
 
     def forward_part(s):
-        def body(r, carry):
+        def body(r):
             at = block(r, blk)
             total = dot_nt(u_b[at, :], w_d[...]) + dot_nt(ctx_s[at, :], w_a[:, 3 * width:])
-            part[0, s, at, :] = total.astype(BF16)
-            return carry
-        lax.fori_loop(0, steps, body, 0)
+            part[0, s % 2, at, :] = total.astype(BF16)
+        loop(steps, body)
 
     def backward_part(s):
-        def body(r, carry):
+        def body(r):
             at = block(r, blk)
             d_h1 = dot_nt(dqkv_s[at, :], w_a[:, :3 * width]).astype(BF16).astype(F32)
             d_h2 = dot_nt(dpre_b[at, :], w_u[...]).astype(BF16).astype(F32)
             xf = x_b[at, :].astype(F32)
             xh, _ = normalise(xf)
-            part[1, s, at, :] = (d_h1 * vecs[0:1, :] + d_h2 * vecs[1:2, :]).astype(BF16)
+            part[1, s % 2, at, :] = (d_h1 * gain1 + d_h2 * gain2).astype(BF16)
             for i, v in enumerate((d_h1 * xh, d_h1, d_h2 * xh, d_h2)):
                 ln_acc[i] += fold(v)
-            return carry
-        lax.fori_loop(0, steps, body, 0)
+        loop(steps, body)
 
     def weight_part():
-        def body(r, carry):
+        def body(r):
             at = block(r, d_loc)
             acc[at, :3 * width] += dot_tn(h1_b[:, at], dqkv_s[...])
             acc[at, 3 * width:] += dot_tn(cot_b[:, at], ctx_s[...])
-            return carry
-        lax.fori_loop(0, n_tx, body, 0)
+        loop(n_tx, body)
 
     def share(a, s):
         for j, yy in enumerate((1 - y, y)):
-            links.send(core_slot[a][j] + s, part.at[a, s, rows(yy * 2 + 1 - core)], rc.at[a, s, yy], core_dev)
+            links.send(core_slot[a][j] + s, part.at[a, s % 2, rows(yy * 2 + 1 - core)], rc.at[a, s, yy], core_dev)
 
     step = 32
 
@@ -482,36 +568,35 @@
         for a in BOTH:
             links.arrive(core_slot[a][0] + s, rc.at[a, s, 1 - y], core_dev)
 
-            def body(r, carry):
+            def body(r):
                 at = block(r, step)
-                mine = part[a, s, pl.ds(pl.multiple_of(t_y * sub + r * step, step), step), :]
+                mine = part[a, s % 2, pl.ds(pl.multiple_of(t_y * sub + r * step, step), step), :]
                 sy[a, s, at, :] = (mine.astype(F32) + rc[a, s, 1 - y, at, :].astype(F32)).astype(BF16)
-                return carry
-            lax.fori_loop(0, sub // step, body, 0)
+            loop(sub // step, body)
             links.send(y_slot[a] + s, sy.at[a, s], ry.at[a, s], y_dev)
 
     def finish(s):
         for a in BOTH:
             links.arrive(core_slot[a][1] + s, rc.at[a, s, y], core_dev)
             links.arrive(y_slot[a] + s, ry.at[a, s], y_dev)
-
-            def body(r, carry):
+            links.sent(y_slot[a] + s, sy.at[a, s])
+
+            def body(r):
                 at = block(r, step)
                 whole = pl.ds(pl.multiple_of(t * sub + r * step, step), step)
-                total = part[a, s, whole, :].astype(F32) + rc[a, s, y, at, :].astype(F32) + ry[a, s, at, :].astype(F32)
-                xf = x_own[s, at, :].astype(F32)
+                total = part[a, s % 2, whole, :].astype(F32) + rc[a, s, y, at, :].astype(F32) + ry[a, s, at, :].astype(F32)
+                xf = x_own[s % 2, at, :].astype(F32)
                 if a == 0:
-                    out = xf + total + vecs[2:3, :]
+                    out = xf + total + bias
                 else:
                     xh, inv = normalise(xf)
-                    out = c_own[s, at, :].astype(F32) + inv * (total - row_mean(total) - xh * row_mean(total * xh))
-                fin[a, s, at, :] = out.astype(BF16)
-                return carry
-            lax.fori_loop(0, sub // step, body, 0)
+                    out = c_own[s % 2, at, :].astype(F32) + inv * (total - row_mean(total) - xh * row_mean(total * xh))
+                sy[a, s, at, :] = out.astype(BF16)
+            loop(sub // step, body)
             place = outs[a].at[z * n_seq + s, rows(t)]
             for k in OTHERS:
-                links.send(z_slot[a][k] + s, fin.at[a, s, :, cols((z + k) % n_tx)], place, z_dev[k])
-            mine = fin.at[a, s, :, cols(z)]
+                links.send(z_slot[a][k] + s, sy.at[a, s, :, cols((z + k) % n_tx)], place, z_dev[k])
+            mine = sy.at[a, s, :, cols(z)]
             pltpu.make_async_copy(mine, place, local_sems.at[9 + a * n_seq + s]).start()
             links.send(ag_y[a][0] + s, mine, place, y_dev)
             links.send(ag_c[a][0][0] + s, mine, place, core_dev)
@@ -534,38 +619,24 @@
                 links.arrive(ag_y[a][k] + s, place, y_dev)
                 links.send(ag_c[a][k][1] + s, place, place, core_dev)
 
+    def core_done(s):
+        for a in BOTH:
+            for j in BOTH:
+                links.sent(core_slot[a][j] + s, sy.at[a, s])
+
     def settle(s):
         for a in BOTH:
             for k in range(n_tx):
+                piece = outs[a].at[src(k) * n_seq + s, rows(t)]
                 for j, who in enumerate((t_core, t_diag)):
                     links.arrive(ag_c[a][k][j] + s, outs[a].at[src(k) * n_seq + s, rows(who)], core_dev)
-            pltpu.make_async_copy(fin.at[a, s, :, cols(z)], outs[a].at[z * n_seq + s, rows(t)], local_sems.at[9 + a * n_seq + s]).wait()
-        done(s)
-
-    def done(s):
-        for a in BOTH:
-            for j, yy in enumerate((1 - y, y)):
-                links.make(core_slot[a][j] + s, part.at[a, s, rows(yy * 2 + 1 - core)], rc.at[a, s, yy], core_dev).wait_send()
-            links.make(y_slot[a] + s, sy.at[a, s], ry.at[a, s], y_dev).wait_send()
-            for k in range(n_tx):
-                mine = fin.at[a, s, :, cols((z + k) % n_tx)]
-                place = outs[a].at[src(k) * n_seq + s, rows(t)]
+                    links.sent(ag_c[a][k][j] + s, piece)
+                links.sent(ag_y[a][k] + s, piece)
                 if k:
-                    links.make(z_slot[a][k] + s, mine, place, z_dev[k]).wait_send()
-                links.make(ag_y[a][k] + s, place, place, y_dev).wait_send()
-                for j in BOTH:
-                    links.make(ag_c[a][k][j] + s, place, place, core_dev).wait_send()
-
-    own_in = [
-        pltpu.make_async_copy(x.at[:, rows(t), :], x_own, local_sems.at[9 + 2 * n_seq]),
-        pltpu.make_async_copy(cot.at[:, rows(t), :], c_own, local_sems.at[10 + 2 * n_seq]),
-    ]
-    for copy in own_in:
-        copy.start()
-    for copy in own_in:
-        copy.wait()
-
-    def one(s, carry):
+                    links.sent(z_slot[a][k] + s, piece)
+            pltpu.make_async_copy(sy.at[a, s, :, cols(z)], outs[a].at[z * n_seq + s, rows(t)], local_sems.at[9 + a * n_seq + s]).wait()
+
+    def one(s):
         for copy in load_early(s):
             copy.wait()
 
@@ -577,8 +648,17 @@
         for copy in load_late(s):
             copy.start()
         attend(s)
+        pl.when(s == 0)(lambda: rs_far(0))
+        pl.when(s == 2)(lambda: rs_far(1))
         for copy in load_late(s):
             copy.wait()
+
+        @pl.when(s == 2)
+        def _():
+            core_done(0)
+
+        x_own[s % 2] = x_b[rows(t), :]
+        c_own[s % 2] = cot_b[rows(t), :]
         forward_part(s)
         share(0, s)
         backward_part(s)
@@ -586,70 +666,77 @@
         weight_part()
         give(s)
 
+        @pl.when(s == 0)
+        def _():
+            rs_start(1)
+            rs_near(0)
+
         @pl.when(s > 0)
         def _():
             finish(s - 1)
 
-        return carry
-
-    lax.fori_loop(0, n_seq, one, 0)
+        pl.when(s == 1)(lambda: rs_end(0))
+
+    rs_start(0)
+    loop(n_seq, one)
+    rs_start(2)
+    forward(0)
+    rs_near(1)
     last = n_seq - 1
-    pw[...] = acc[...].astype(BF16)
-    for k in OTHERS:
-        links.send(rs_slot[k], pw.at[cols((z + k) % n_tx)], dw_buf.at[k - 1], z_dev[k])
+    MINE, CORE, PAIR, FROM_Y, QUAD = range(5)
+    sm_buf[MINE] = small[...]
     for i in range(4):
-        sm_buf[0, i:i + 1, :] = ln_acc[i].sum(0, keepdims=True)
-    sm_buf[0, 4:5, :] = small[4:5, :]
-    sm_buf[0, 5:6, 0:3 * width] = dbq[...].sum(0, keepdims=True)
-    sm_buf[0, 5:6, 3 * width:] = jnp.zeros((1, d_model - 3 * width), F32)
-    sm_buf[0, 6:8, :] = jnp.zeros((2, d_model), F32)
-    links.send(sm_slot[0], sm_buf.at[0], sm_buf.at[1], core_dev)
-    row = lax.broadcasted_iota(jnp.int32, (8, d_model), 0)
-    forward(0)
+        sm_buf[MINE, i:i + 1, :] = jnp.sum(ln_acc[i], axis=0, keepdims=True)
+    sm_buf[MINE, 5:6, :3 * width] = jnp.sum(dbq[...], axis=0, keepdims=True)
+    links.send(sm_slot[0], sm_buf.at[MINE], sm_buf.at[CORE], core_dev)
+    over_ty = (lax.broadcasted_iota(jnp.int32, small.shape, 0) < 4).astype(F32)
     finish(last)
-    links.arrive(sm_slot[0], sm_buf.at[1], core_dev)
-    sm_buf[2] = sm_buf[0] + jnp.where(row < 4, sm_buf[1], 0.0)
-    links.send(sm_slot[1], sm_buf.at[2], sm_buf.at[3], y_dev)
+    links.arrive(sm_slot[0], sm_buf.at[CORE], core_dev)
+    sm_buf[PAIR] = sm_buf[MINE] + over_ty * sm_buf[CORE]
+    links.send(sm_slot[PAIR], sm_buf.at[PAIR], sm_buf.at[FROM_Y], y_dev)
     forward(1)
     forward_y(0)
-    links.arrive(sm_slot[1], sm_buf.at[3], y_dev)
-    sm_buf[4] = sm_buf[2] + jnp.where(row < 4, sm_buf[3], 0.0)
+    links.arrive(sm_slot[PAIR], sm_buf.at[FROM_Y], y_dev)
+    sm_buf[QUAD] = sm_buf[PAIR] + over_ty * sm_buf[FROM_Y]
     for k in OTHERS:
-        links.send(sm_slot[1 + k], sm_buf.at[4], sm_buf.at[4 + k], z_dev[k])
+        links.send(sm_slot[QUAD + k], sm_buf.at[QUAD], sm_buf.at[QUAD + k], z_dev[k])
+    rs_far(2)
+    rs_end(1)
     forward(last)
     forward_y(1)
+    rs_near(2)
     forward_y(last)
+    rs_end(2)
     for k in OTHERS:
-        links.arrive(rs_slot[k], dw_buf.at[k - 1], y_dev)
-    dw_out[...] = acc[cols(z), :]
-    for k in OTHERS:
-        dw_out[...] += dw_buf[k - 1].astype(F32)
-    for k in OTHERS:
-        links.arrive(sm_slot[1 + k], sm_buf.at[4 + k], y_dev)
-    small_out[...] = sm_buf[4] + sm_buf[5] + sm_buf[6] + sm_buf[7]
+        links.arrive(sm_slot[QUAD + k], sm_buf.at[QUAD + k], y_dev)
+    small_out[...] = jnp.sum(sm_buf[QUAD:], axis=0)
     for s in range(n_seq):
         settle(s)
-    for k in OTHERS:
-        links.make(rs_slot[k], pw.at[cols((z + k) % n_tx)], dw_buf.at[k - 1], z_dev[k]).wait_send()
-        links.make(sm_slot[1 + k], sm_buf.at[4], sm_buf.at[4 + k], z_dev[k]).wait_send()
-    links.make(sm_slot[0], sm_buf.at[0], sm_buf.at[1], core_dev).wait_send()
-    links.make(sm_slot[1], sm_buf.at[2], sm_buf.at[3], y_dev).wait_send()
-
-
-def layer_tail(qkv, d_ctx, u, d_pre, h1, x, cot, w_d, w_a, w_u, vecs, small, n_tx, n_ty):
+        if s:
+            core_done(s)
+    for w, slots in enumerate(rs_slot):
+        for name, cond in ((R0, z < end), (L0, z > 0), (R1, lower), (L1, ~lower), (FAR, first | last_z)):
+            links.sent(slots[name], arrivals[w].at[name], cond)
+    for i in (MINE, PAIR, *[QUAD + k for k in OTHERS]):
+        links.sent(sm_slot[i], sm_buf.at[MINE])
+
+
+def layer_tail(qkv, d_ctx, u, d_pre, h1, x, cot, w_d, w_a, w_u, p_down, p_up, vecs, small, n_tx, n_ty):
     n_seq, seq, d_model = x.shape
+    end = n_tx - 1
     width, d_loc, blk, sub = d_ctx.shape[-1], d_model // n_tx, 256, seq // n_ty
     any_spec, vmem = pl.BlockSpec(memory_space=pl.ANY), pl.BlockSpec(memory_space=pltpu.VMEM)
     out = jax.ShapeDtypeStruct((n_seq * n_tx, seq, d_loc), BF16)
     cos_tab, sin_tab = rope_tables(seq, width)
-    slots = n_seq * 2 * (3 + 4 * n_tx) + 5 + n_tx
+    shapes = (p_down.shape[1:], p_up.shape[1:], (d_loc, d_model))
+    slots = n_seq * 2 * (3 + 4 * n_tx) + 5 * 5
     wide = lambda *lead: pltpu.VMEM(lead + (seq, d_model), BF16)
     piece = lambda *lead: pltpu.VMEM(lead + (sub, d_model), BF16)
     return pl.pallas_call(
         functools.partial(tail_kernel, n_tx=n_tx, blk=blk),
-        in_specs=[any_spec] * 7 + [vmem] * 8,
-        out_specs=[any_spec, any_spec, vmem, vmem],
-        out_shape=[out, out, jax.ShapeDtypeStruct((8, d_model), F32), jax.ShapeDtypeStruct((d_loc, d_model), F32)],
+        in_specs=[any_spec] * 7 + [vmem] * 3 + [any_spec] * 2 + [vmem] * 5,
+        out_specs=[any_spec] * 2 + [vmem] * 4,
+        out_shape=[out, out, *[jax.ShapeDtypeStruct(shape, F32) for shape in (small.shape, *shapes)]],
         scratch_shapes=[
             pltpu.VMEM((2, seq, 3 * width), BF16),
             pltpu.VMEM((2, seq, width), BF16),
@@ -662,24 +749,23 @@
             pltpu.VMEM((d_model, d_model), F32),
             pltpu.VMEM((8, 3 * width), F32),
             pltpu.VMEM((4, 8, d_model), F32),
-            pltpu.VMEM((d_model, d_model), BF16),
-            pltpu.VMEM((n_tx - 1, d_loc, d_model), BF16),
-            wide(2, n_seq),
+            *[pltpu.VMEM((n,) + shape, BF16) for n, shape in zip((5, 5, 5, 2, 2), shapes + shapes)],
+            wide(2, 2),
             piece(2, n_seq, 2),
             piece(2, n_seq),
             piece(2, n_seq),
-            piece(2, n_seq),
-            piece(n_seq),
-            piece(n_seq),
+            piece(2),
+            piece(2),
             pltpu.VMEM((8, 8, d_model), F32),
             pltpu.SemaphoreType.DMA((slots,)),
             pltpu.SemaphoreType.DMA((slots,)),
-            pltpu.SemaphoreType.DMA((11 + 2 * n_seq,)),
+            pltpu.SemaphoreType.DMA((9 + 2 * n_seq,)),
+            pltpu.SemaphoreType.DMA((2, 2)),
         ],
         compiler_params=pltpu.CompilerParams(collective_id=1, has_side_effects=True, vmem_limit_bytes=67_000_000),
         cost_estimate=pl.CostEstimate(flops=60_000_000_000, bytes_accessed=60_000_000, transcendentals=0),
         name="layer_tail",
-    )(qkv, d_ctx, u, d_pre, h1, x, cot, w_d, w_a, w_u, vecs, small, cos_tab, sin_tab, rope_turn(width))
+    )(qkv, d_ctx, u, d_pre, h1, x, cot, w_d, w_a, w_u, p_down, p_up, vecs, small, cos_tab, sin_tab, rope_turn(width))
 
 
 def solution(mesh):
@@ -702,27 +788,20 @@
         vec_loc = jnp.stack([ln1_gain, ln1_bias, ln2_gain, ln2_bias, b_dense, b_down], axis=0)
         vec_loc = jnp.pad(vec_loc, ((0, 10), (0, 0)))
         bq = b_qkv.astype(F32).reshape(heads, 3, HEAD).transpose(1, 0, 2).reshape(1, 3 * hw)
-        row8 = lambda a: jnp.pad(a, ((0, 7), (0, 0)))
         x, cot, w_u, w_dt, w_a, vecs, h1, qkv, u, d_pre, d_ctx, part_down, part_up, d_bup = layer_front(
-            x_act, cot_out, w_up, w_down.T, jnp.concatenate([wq_loc, w_dense.T], axis=1), vec_loc, row8(bq), row8(b_up.astype(F32)[None]), n_tx, n_ty)
+            x_act, cot_out, w_up, w_down.T, jnp.concatenate([wq_loc, w_dense.T], axis=1), vec_loc, bq, b_up.astype(F32)[None], n_tx, n_ty)
         g1, g2, b_o, b_d = [vecs[i].astype(F32) for i in (0, 2, 4, 5)]
 
-        def scatter_grad(part):
-            return lax.psum_scatter(part, 'tx', scatter_dimension=0, tiled=True)
-
-        sum_down, sum_up = scatter_grad(part_down), scatter_grad(part_up)
-        d_w_down, d_w_up = sum_down.astype(F32).T, sum_up.astype(F32)
         d_b_up = d_bup.sum(0)
         small = jnp.pad(d_b_up[None], ((4, 3), (0, d_model - d_b_up.shape[0])))
         rows = jnp.pad(jnp.stack([g1, g2, b_o + b_d], axis=0), ((0, 5), (0, 0)))
         by_seq = lambda a: a.reshape(n_b, seq, a.shape[-1])
-        y_out, dx_act, total, d_w_a = layer_tail(by_seq(qkv), by_seq(d_ctx), by_seq(u), by_seq(d_pre), by_seq(h1), by_seq(x), by_seq(cot), w_dt, w_a, w_u, rows, small, n_tx, n_ty)
+        y_out, dx_act, total, d_w_down, d_w_up, d_w_a = layer_tail(by_seq(qkv), by_seq(d_ctx), by_seq(u), by_seq(d_pre), by_seq(h1), by_seq(x), by_seq(cot), w_dt, w_a, w_u, part_down, part_up, rows, small, n_tx, n_ty)
         d_w_qkv = d_w_a[:, :3 * hw].reshape(d_loc, 3, heads, HEAD).transpose(0, 2, 1, 3).reshape(d_loc, heads, 3 * HEAD)
         d_w_dense = d_w_a[:, 3 * hw:].T
         ln_sum = lax.dynamic_slice(total, (0, z * d_loc), (4, d_loc))
-        d_b_up = total[4, :d_b_up.shape[0]]
-        d_b_qkv = total[5, :3 * hw].reshape(3, heads, HEAD).transpose(1, 0, 2).reshape(heads, 3 * HEAD)
+        d_b_up, d_b_qkv = total[4, :d_b_up.shape[0]], total[5, :3 * hw].reshape(3, heads, HEAD).transpose(1, 0, 2).reshape(heads, 3 * HEAD)
         d_b_out = cot_out.astype(F32).sum((0, 1))
-        return (y_out, dx_act, ln_sum[0], ln_sum[1], ln_sum[2], ln_sum[3], d_w_qkv, d_b_qkv, d_w_dense, d_b_out, d_w_up, d_b_up, d_w_down, d_b_out)
+        return (y_out, dx_act, *ln_sum, d_w_qkv, d_b_qkv, d_w_dense, d_b_out, d_w_up, d_b_up, d_w_down, d_b_out)
 
     return jax.shard_map(body, mesh=mesh, in_specs=in_specs, out_specs=out_specs, check_vma=False)

time: 375 us -> 336 us (0.90)
  Pallas kernels: 317 us -> 296 us
  between operations: 14.2 us -> 0.78 us
    pallas_call x1, Pallas kernels: 185 us -> 163 us  [layer_tail(): pl.pallas_call(functools.partial(tail_kernel, n_tx=n_tx, blk=blk), in_spe...]
    unnamed x17 -> x20, local copies, waits for them, and re-layouts: 12.8 us -> 10.9 us
  transfers between devices with their start and end apart: 2 -> 0, of which waited for: 0 -> 0; matrix products, arithmetic and copies ran while one was open for 5% -> 0% of each run, Pallas kernels for 50% -> 0%
where the time goes in v1:
time: 336 us; the launch traced here: 335 us
  Pallas kernels  296 us (88%)
  local copies, waits for them, and re-layouts  28.9 us (9%)
  other arithmetic  9.78 us (3%)
    pallas_call x1, Pallas kernels, layer_tail(): pl.pallas_call(functools.partial(tail_kernel, n_tx=n_tx, blk=blk), in_spe...  163 us
    pallas_call x1, Pallas kernels, layer_front(): pl.pallas_call(functools.partial(front_kernel, n_tx=n_tx, n_ty=n_ty, blk=...  132 us
    unnamed x20, local copies, waits for them, and re-layouts  10.9 us

profile of v1, /device:TPU:0, one launch (start us, length us, event | category | flops | bytes accessed | tf_op | source)
XLA Modules:
  0.0 335.4 jit_solution(1518161654132884821)
XLA Ops:
  0.6 1.0 copy.45
  1.7 0.2 copy.47
  1.8 1.0 copy.46
  2.9 0.9 pad_maximum_fusion.wa_in
  3.7 2.0 copy.44
  5.8 0.7 stack.27
  6.4 0.7 stack.28
  7.1 0.7 stack.29
  7.7 0.7 stack.30
  8.4 0.7 stack.31
  9.1 0.7 stack.32
  9.7 0.6 pad.20.v_in
  10.3 0.8 reshape.116
  11.1 0.7 reshape.112.b_qkv
  11.8 1.3 broadcast_in_dim.13
  13.1 132.4 %layer_front.1 = (bf16[2304,1024]{1,0:T(8,128)(2,1)}, bf16[2304,1024]{1,0:T(8,128)(2,1)}, bf16[1024,1024]{1,0:T(8,128)(2,1)}, bf16[1024,1024]{1,0:T(8,128)(2,1)}...) custom-call(bf16[4,4,576,256]{3,2,1,0:T(8,128)(2,1)} %bitcast.54, ...), custom_call_target="tpu_custom_call" | custom-call | flops 60000002048 | bytes 60000000 | tf_op jit(solution)/shard_map/layer_front/pallas_call | solution.py:337
  145.5 0.8 slice_convert_fusion.1
  146.3 0.8 convert_add_fusion
  147.1 0.6 select_maximum_fusion.vecs
  147.7 0.8 reduce_sum.18
  148.5 0.6 pad.22.small
  149.1 0.7 subtract_convert_fusion.turn_tab
  149.9 0.1 iota_multiply_fusion
  149.9 0.1 fusion.3
  150.1 0.1 tile.8
  150.1 1.1 copy.49.cos_tab
  151.3 0.1 tile.20
  151.4 1.1 copy.50.sin_tab
  152.5 163.5 %layer_tail.1 = (bf16[12,768,256]{2,1,0:T(8,128)(2,1)}, bf16[12,768,256]{2,1,0:T(8,128)(2,1)}, f32[8,1024]{1,0:T(8,128)}, f32[1024,256]{1,0:T(8,128)}, f32[256,1024]{1,0:T(8,128)}, /*index=5*/f32[256,1024]{1,0:T(8,128)}) custom-call(bf16[3,768,768]{2,1,0:T(8,128)(2,1)} %bitcast.60, bf16[3,768,256]{2,1,0:T(8,128)(2,1)} %bitcast.61, ...), custom_call_target="tpu_custom_call" | custom-call | flops 60000002048 | bytes 60000000 | tf_op jit(solution)/shard_map/layer_tail/pallas_call | solution.py:735
  316.0 1.2 slice.28
  317.2 0.3 copy.51
  317.5 1.0 copy.52
  318.4 1.0 slice_bitcast_fusion
  319.4 0.8 copy.54
  320.2 0.8 slice_reduce_fusion
  321.0 0.1 reshape_squeeze.3
  321.1 0.7 reshape.110
  321.7 0.0 copy-start
  321.8 1.5 fusion.6
  323.3 1.4 slice.31
  324.6 0.0 slice-start
  324.7 3.7 %convert_reduce_fusion = f32[256]{0:T(256)S(1)} fusion(bf16[12,768,256]{2,1,0:T(8,128)(2,1)} %param.15), kind=kLoop, calls=%fused_computation | loop fusion | flops 4718336 | bytes 4719616 | tf_op jit(solution)/shard_map/reduce_sum | solution.py:804
  328.4 0.0 copy-start.3
  328.4 0.6 copy.62
  328.9 0.0 copy-done
  328.9 0.0 slice-start.1
  328.9 2.2 copy.63
  331.1 0.0 copy-done.3
  331.1 0.0 slice-done
  331.1 0.0 slice-done.1
  331.1 0.0 copy-start.2
  331.1 0.0 copy-start.1
  331.2 2.3 copy.64
  333.5 0.0 copy-done.2
  333.5 1.0 copy.65
  334.4 0.0 copy-done.1
  334.4 1.0 copy.66
  (10 shorter events, 0.1 us)
Async XLA Ops:
  321.7 7.2 %copy-start = (bf16[12,768,256]{2,1,0:T(8,128)(2,1)S(1)}, bf16[12,768,256]{2,1,0:T(8,128)(2,1)}, u32[]{:S(2)}) copy-start(bf16[12,768,256]{2,1,0:T(8,128)(2,1)} %get-tuple-element.150) | copy-start | bytes 14155780
  324.6 6.5 %slice-start = ((s8[4718592]{0:T(1024)(128)(4,1)}), s8[4194304]{0:T(1024)(128)(4,1)S(1)}, s32[]{:S(2)}) async-start(s8[4718592]{0:T(1024)(128)(4,1)} %bitcast.35), calls=%async_computation | async-start | bytes 8388608
  328.4 2.8 copy-start.3
  328.9 2.2 slice-start.1
  331.1 2.3 copy-start.2
  331.1 3.3 copy-start.1

commit v2 on v1

--- a/solution.py
+++ b/solution.py
@@ -1,6 +1,7 @@
 import functools
 import jax
 import jax.numpy as jnp
+import numpy as np
 from jax import lax
 from jax.experimental import pallas as pl
 from jax.experimental.pallas import tpu as pltpu
@@ -14,22 +15,21 @@
 BF16 = jnp.bfloat16
 
 def rope_tables(seq_len, width):
-    inv_freq = ROPE_BASE ** (-jnp.arange(0, ROT, 2, dtype=F32) / ROT)
-    angles = jnp.arange(seq_len, dtype=F32)[:, None] * inv_freq[None, :]
-    angles = jnp.concatenate([angles, angles], axis=-1)
-    pad = ((0, 0), (0, HEAD - ROT))
-    cos_head = jnp.pad(jnp.cos(angles), pad, constant_values=1.0)
-    sin_head = jnp.pad(jnp.sin(angles), pad)
-    return jnp.tile(cos_head, (1, width // HEAD)), jnp.tile(sin_head, (1, width // HEAD))
+    inv_freq = (ROPE_BASE ** (-np.arange(0, ROT, 2, dtype=np.float32) / ROT)).astype(np.float32)
+    angles = np.arange(seq_len, dtype=np.float32)[:, None] * inv_freq[None]
+    angles = np.concatenate([angles, angles, np.zeros((seq_len, HEAD - ROT), np.float32)], axis=1)
+    angles = np.tile(angles, (1, width // HEAD)).astype(np.float64)
+    return np.cos(angles).astype(np.float32), np.sin(angles).astype(np.float32)
 
 
 def rope_turn(width):
-    row = lax.broadcasted_iota(jnp.int32, (width, width), 0)
-    col = lax.broadcasted_iota(jnp.int32, (width, width), 1)
-    lane = col % HEAD
-    minus = (row == col + ROT // 2) & (lane < ROT // 2)
-    plus = (row == col - ROT // 2) & (lane >= ROT // 2) & (lane < ROT)
-    return (plus.astype(F32) - minus.astype(F32)).astype(BF16)
+    turn = np.zeros((width, width), np.float32)
+    for lane in range(width):
+        place = lane % HEAD
+        if place < ROT:
+            lower = place < ROT // 2
+            turn[lane + ROT // 2 if lower else lane - ROT // 2, lane] = -1.0 if lower else 1.0
+    return turn.astype(BF16)
 
 
 def dot_nn(a, b):
@@ -117,9 +117,9 @@
 
 
 def front_kernel(
-    x_in, c_in, wu_in, wd_in, wa_in, v_in, b_qkv, b_up,
-    x_out, c_out, wu_out, wd_out, wa_out, v_out, h1_out, qkv_out, u_out, dpre_out, dctx_out, dwd_out, dwu_out, dbup_out,
-    x_v, c_v, wu_v, wd_v, wa_v, h1_v, h2_v, u_v, gp_v, qkv_v, dpre_v, dctx_v, dwd_v, dwu_v,
+    x_in, c_in, wu_in, wd_in, wa_in, v0, v1, v2, v3, v4, v5, b_qkv, b_up,
+    x_out, c_out, wu_out, wd_out, wa_out, v_out, h1_out, qkv_out, u_out, dpre_out, dctx_out, dwd_out, dwu_out, sums_out,
+    v_in, x_v, c_v, wu_v, wd_v, wa_v, h1_v, h2_v, u_v, gp_v, qkv_v, dpre_v, dctx_v, dwd_v, dwu_v,
     send_sems, recv_sems, local_sems, out_sems, *, n_tx, n_ty, blk,
 ):
     g, z, t, core, y, t_core, t_y, t_diag = neighbours()
@@ -143,9 +143,13 @@
     def w_rows(s, group):
         return pl.ds(pl.multiple_of(s * d_loc + group * half, half), half)
 
-    own = [pltpu.make_async_copy(v_in, v_out.at[:, cols(z)], local_sems.at[0])]
-    for i, (src, dst) in enumerate(((wu_in, wu_v), (wa_in, wa_v), (wd_in, wd_v))):
-        own.append(pltpu.make_async_copy(src, dst.at[cols(z), :], local_sems.at[1 + i]))
+    v_in[...] = jnp.zeros_like(v_in)
+    for i, v in enumerate((v0, v1, v2, v3, v4, v5)):
+        v_in[i:i + 1, :] = v[...].astype(F32).reshape(1, d_loc)
+    v_out[:, cols(z)] = v_in[...]
+    own = []
+    for i, (src, dst) in enumerate(((wu_in, wu_v.at[cols(z), :]), (wd_in, wd_v.at[:, cols(z)]), (wa_in, wa_v.at[cols(z), :]))):
+        own.append(pltpu.make_async_copy(src, dst, local_sems.at[1 + i]))
     for i, (src, dst) in enumerate(((x_in, x_v), (c_in, c_v))):
         for c in range(n_ty):
             own.append(pltpu.make_async_copy(src.at[z, c], dst.at[pl.ds(c * chunk, chunk), cols(z)], local_sems.at[4 + i * n_ty + c]))
@@ -153,35 +157,36 @@
         copy.start()
     enter([core_dev, y_dev, x_dev] + z_dev[1:])
 
-    weights = ((wu_in, wu_v), (wa_in, wa_v), (wd_in, wd_v))
+    mine = block(g, half)
+    weights = (
+        (wu_in.at[mine, :], lambda s, group: wu_v.at[w_rows(s, group), :]),
+        (wd_in.at[:, mine], lambda s, group: wd_v.at[:, w_rows(s, group)]),
+        (wa_in.at[mine, :], lambda s, group: wa_v.at[w_rows(s, group), :]),
+    )
+    UP, DOWN, ATTN = range(len(weights))
     w_slot = [[links.slot() for _ in range(2 * n_tx)] for _ in weights]
     x_slot = [[links.slot() for _ in range(n_tx)] for _ in weights]
 
-    def w_send(w, hops, src):
-        s_left, s_right = z - hops, z + hops
-        links.send(w_slot[w][hops + 1], src(s_left), weights[w][1].at[w_rows(s_left, g), :], right, (s_left >= 0) & (z < end))
-        links.send(w_slot[w][n_tx + hops + 1], src(s_right), weights[w][1].at[w_rows(s_right, g), :], left, (s_right < n_tx) & (z > 0))
-
-    def w_start(w):
-        mine = weights[w][0].at[block(g, half), :]
-        w_send(w, 0, lambda s: mine)
+    def w_send(w, hops):
+        own_half, place = weights[w]
+        for slot, s, to, ok in ((hops, z - hops, right, (z >= hops) & (z < end)), (n_tx + hops, z + hops, left, (z + hops < n_tx) & (z > 0))):
+            links.send(w_slot[w][slot + 1], place(s, g) if hops else own_half, place(s, g), to, ok)
 
     def w_sides(hops):
-        return (hops, hops, z - hops, z - hops >= 0), (n_tx + hops, n_tx - hops, z + hops, z + hops < n_tx)
+        return (hops, hops, z - hops, z >= hops), (n_tx + hops, n_tx - hops, z + hops, z + hops < n_tx)
 
     def w_pass(w, hops):
-        out = weights[w][1]
         for slot, x_at, s, ok in w_sides(hops):
-            place = out.at[w_rows(s, g), :]
+            place = weights[w][1](s, g)
             links.arrive(w_slot[w][slot], place, right, ok)
             links.send(x_slot[w][x_at], place, place, x_dev, ok)
         if hops < end:
-            w_send(w, hops, lambda s: out.at[w_rows(s, g), :])
+            w_send(w, hops)
 
     def w_finish(w):
-        for hops in OTHERS:
+        for hops in range(1, n_tx):
             for slot, x_at, s, ok in w_sides(hops):
-                links.arrive(x_slot[w][x_at], weights[w][1].at[w_rows(s, 1 - g), :], x_dev, ok)
+                links.arrive(x_slot[w][x_at], weights[w][1](s, 1 - g), x_dev, ok)
 
     arrays = ((x_in, x_v), (c_in, c_v))
     z_slot = [[links.slot() for _ in range(n_tx)] for _ in arrays]
@@ -192,8 +197,8 @@
     def src_cols(k):
         return cols((z + n_tx - k) % n_tx)
 
-    def t_start(a):
-        for k in OTHERS:
+    def t_send(a, *which):
+        for k in which:
             links.send(z_slot[a][k], arrays[a][0].at[(z + k) % n_tx, t], arrays[a][1].at[rows(t), cols(z)], z_dev[k])
 
     def t_pass(a, k):
@@ -212,25 +217,22 @@
             for j, c in enumerate((t_core, t_diag)):
                 links.arrive(c_slot[a][k][j], arrays[a][1].at[rows(c), src_cols(k)], core_dev)
 
-    for w in BOTH:
-        w_start(w)
+    X, COT = BOTH
+    w_send(UP, 0)
     for k in OTHERS:
         links.send(v_slot[k], v_in, v_out.at[:, cols(z)], z_dev[k])
-    t_start(0)
-    for w in BOTH:
-        w_pass(w, 1)
+    t_send(X, *OTHERS)
+    w_pass(UP, 1)
     for k in OTHERS:
-        t_pass(0, k)
-    for w in BOTH:
-        w_pass(w, 2)
-    w_start(2)
-    t_start(1)
+        t_pass(X, k)
+    w_pass(UP, 2)
+    w_send(DOWN, 0)
+    t_send(COT, 2)
     for k in OTHERS:
-        t_pass_y(0, k)
-    for w in BOTH:
-        w_pass(w, 3)
-        w_finish(w)
-    t_finish(0)
+        t_pass_y(X, k)
+    w_pass(UP, 3)
+    w_finish(UP)
+    t_finish(X)
     for k in OTHERS:
         links.arrive(v_slot[k], v_out.at[:, src_cols(k)], y_dev)
     for copy in own:
@@ -245,14 +247,14 @@
 
     write(x_v, x_out)
     write(wu_v, wu_out)
-    write(wa_v, wa_out)
-
-    def tokens(step):
-        for k in OTHERS:
-            step(1, k)
-
-    late_steps = tuple(enumerate((lambda: w_pass(2, 1), None, lambda: tokens(t_pass), lambda: w_pass(2, 2), lambda: tokens(t_pass_y), None, lambda: w_pass(2, 3))))
-    vec = v_out[...].astype(F32)
+
+    def early():
+        w_pass(DOWN, 1)
+        t_send(COT, 1)
+        w_send(ATTN, 0)
+        t_send(COT, 3)
+
+    vec = v_out[...]
     g1, be1, g2, be2 = [vec[i:i + 1] for i in range(4)]
 
     def forward(i):
@@ -263,37 +265,41 @@
         h2 = (xh * g2 + be2).astype(BF16)
         h1_v[at, :] = h1
         h2_v[at, :] = h2
-        qkv_v[at, :] = (dot_nn(h1, wa_v[:, :3 * width]) + b_qkv[...]).astype(BF16)
-        pre = (dot_nn(h2, wu_v[...]) + b_up[...]).astype(BF16).astype(F32)
+        pre = (dot_nn(h2, wu_v[...]) + b_up[...].astype(F32).reshape(1, -1)).astype(BF16).astype(F32)
         cdf = 0.5 * (1.0 + lax.erf(pre * (0.5 ** 0.5)))
         u_v[at, :] = (pre * cdf).astype(BF16)
         gp_v[at, :] = cdf + pre * (jnp.exp(-0.5 * pre * pre) * (1.0 / (2.0 * jnp.pi) ** 0.5))
-        for when, what in late_steps:
-            if what:
-                pl.when(i == when)(what)
+        pl.when(i == 0)(early)
+        pl.when(i == 4)(lambda: w_pass(DOWN, 2))
 
     loop(tok // blk, forward)
     write(h1_v, h1_out)
-    write(qkv_v, qkv_out)
     write(u_v, u_out)
-    w_finish(2)
-    t_finish(1)
+    t_pass(COT, 2)
+    t_pass(COT, 1)
+    w_pass(ATTN, 1)
+    t_pass(COT, 3)
+    w_pass(DOWN, 3)
+    for k in (2, 1, 3):
+        t_pass_y(COT, k)
+    w_finish(DOWN)
+    t_finish(COT)
     write(c_v, c_out)
     write(wd_v, wd_out)
-    dbup_out[...] = jnp.zeros_like(dbup_out)
+    sums_out[...] = jnp.zeros_like(sums_out)
 
     def backward(i):
         at = block(i, blk)
         cot = c_v[at, :]
-        d_gelu = dot_nn(cot, wd_v[...]).astype(BF16).astype(F32)
+        d_gelu = dot_nt(cot, wd_v[...]).astype(BF16).astype(F32)
         d_pre = (d_gelu * gp_v[at, :]).astype(BF16)
         dpre_v[at, :] = d_pre
-        dbup_out[...] += fold(d_pre.astype(F32))
-        dctx_v[at, :] = dot_nn(cot, wa_v[:, 3 * width:]).astype(BF16)
+        sums_out[0] += fold(d_pre.astype(F32))
+        sums_out[1] += fold(cot.astype(F32))
+        pl.when(i == 4)(lambda: w_pass(ATTN, 2))
 
     loop(tok // blk, backward)
     write(dpre_v, dpre_out)
-    write(dctx_v, dctx_out)
 
     def down(r):
         dwd_v[r] = dot_tn(u_v[...], c_v[:, cols(r)]).astype(BF16)
@@ -301,23 +307,34 @@
     def up(r):
         dwu_v[r] = dot_tn(h2_v[:, cols(r)], dpre_v[...]).astype(BF16)
 
+    def attn(i):
+        at = block(i, blk)
+        qkv_v[at, :] = (dot_nn(h1_v[at, :], wa_v[:, :3 * width]) + b_qkv[...]).astype(BF16)
+        dctx_v[at, :] = dot_nn(c_v[at, :], wa_v[:, 3 * width:]).astype(BF16)
+
     loop(n_tx, down)
     write(dwd_v, dwd_out)
+    w_pass(ATTN, 3)
     loop(n_tx, up)
     write(dwu_v, dwu_out)
+    w_finish(ATTN)
+    write(wa_v, wa_out)
+    loop(tok // blk, attn)
+    write(qkv_v, qkv_out)
+    write(dctx_v, dctx_out)
     piece = x_v.at[pl.ds(0, chunk), pl.ds(0, d_loc)]
     for a in BOTH:
         for k in OTHERS:
             for slot in (z_slot[a][k], y_slot[a][k], *c_slot[a][k]):
                 links.sent(slot, piece)
     for w in range(len(weights)):
-        shard = weights[w][1].at[pl.ds(0, half), :]
+        shard = weights[w][0]
         for hops in range(n_tx):
             if hops:
                 for _, x_at, _, ok in w_sides(hops):
                     links.sent(x_slot[w][x_at], shard, ok)
             if hops < end:
-                links.sent(w_slot[w][hops + 1], shard, (z - hops >= 0) & (z < end))
+                links.sent(w_slot[w][hops + 1], shard, (z >= hops) & (z < end))
                 links.sent(w_slot[w][n_tx + hops + 1], shard, (z + hops < n_tx) & (z > 0))
     for k in OTHERS:
         links.sent(v_slot[k], v_in)
@@ -325,7 +342,7 @@
         copy.wait()
 
 
-def layer_front(x_act, cot_out, w_up, w_dt, w_a, vecs, b_qkv, b_up, n_tx, n_ty):
+def layer_front(x_act, cot_out, w_up, w_down, w_a, vecs, b_qkv, b_up, n_tx, n_ty):
     batch, seq, d_loc = x_act.shape
     tok = batch * seq // n_tx
     d_model, ff, width, blk = d_loc * n_tx, w_up.shape[1], b_qkv.shape[1] // 3, 256
@@ -336,15 +353,16 @@
     split = lambda a: a.reshape(n_tx, n_ty, tok // n_ty, d_loc)
     return pl.pallas_call(
         functools.partial(front_kernel, n_tx=n_tx, n_ty=n_ty, blk=blk),
-        in_specs=[any_spec] * 6 + [vmem] * 2,
+        in_specs=[any_spec] * 5 + [vmem] * 8,
         out_specs=[any_spec] * 5 + [vmem] + [any_spec] * 7 + [vmem],
         out_shape=[
-            arr(tok, d_model), arr(tok, d_model), arr(d_model, ff), arr(d_model, ff), arr(d_model, 4 * width), arr(vecs.shape[0], d_model),
+            arr(tok, d_model), arr(tok, d_model), arr(d_model, ff), arr(ff, d_model), arr(d_model, 4 * width), jax.ShapeDtypeStruct((8, d_model), F32),
             arr(tok, d_model), arr(tok, 3 * width), arr(tok, ff), arr(tok, ff), arr(tok, width), arr(n_tx, ff, d_loc), arr(n_tx, d_loc, ff),
-            jax.ShapeDtypeStruct((8, ff), F32),
+            jax.ShapeDtypeStruct((2, 8, ff), F32),
         ],
         scratch_shapes=[
-            buf(tok, d_model), buf(tok, d_model), buf(d_model, ff), buf(d_model, ff), buf(d_model, 4 * width),
+            pltpu.VMEM((8, d_loc), F32),
+            buf(tok, d_model), buf(tok, d_model), buf(d_model, ff), buf(ff, d_model), buf(d_model, 4 * width),
             buf(tok, d_model), buf(tok, d_model), buf(tok, ff), pltpu.VMEM((tok, ff), F32), buf(tok, 3 * width), buf(tok, ff), buf(tok, width),
             buf(n_tx, ff, d_loc),
             buf(n_tx, d_loc, ff),
@@ -356,11 +374,11 @@
         compiler_params=pltpu.CompilerParams(collective_id=0, has_side_effects=True, vmem_limit_bytes=67_000_000),
         cost_estimate=pl.CostEstimate(flops=60_000_000_000, bytes_accessed=60_000_000, transcendentals=0),
         name="layer_front",
-    )(split(x_act), split(cot_out), w_up, w_dt, w_a, vecs, b_qkv, b_up)
+    )(split(x_act), split(cot_out), w_up, w_down, w_a, *vecs, b_qkv, b_up)
 
 
 def tail_kernel(
-    qkv, d_ctx, u, d_pre, h1, x, cot, w_d, w_a, w_u, p_down, p_up, vecs, small, cos_tab, sin_tab, turn_tab,
+    qkv, d_ctx, u, d_pre, h1, x, cot, w_d, w_a, w_u, p_down, p_up, vecs, sums, cos_tab, sin_tab, turn_tab,
     y_out, dx_out, small_out, d_down, d_up, d_a,
     qkv_b, dctx_b, u_b, dpre_b, h1_b, x_b, cot_b, q_s, k_s, dq_s, ctx_s, dqkv_s, acc, dbq, ln_acc, arr_down, arr_up, arr_a, own_down, own_up,
     part, rc, sy, ry, x_own, c_own, sm_buf, send_sems, recv_sems, local_sems, rs_sems, *, n_tx, blk,
@@ -437,9 +455,9 @@
                 arrivals[w][move_from, at, :] = (arrivals[w][move_from, at, :].astype(F32) + mine).astype(BF16)
             loop(4, body)
 
-    def rs_start(w):
+    def rs_start(w, *hops):
         for way, near, cond, to in ((1, (R0, R1, FAR), first, right), (-1, (L0, L1, FAR), last_z, left)):
-            for hop in (2, 1, 0):
+            for hop in hops:
                 d, name = z + way * (hop + 1), near[hop]
                 if w >= len(owners):
                     @pl.when(cond)
@@ -483,11 +501,13 @@
         rs_load(w, 0, (end) * (1 - z // 2)).start()
         rs_load(w, 1, (z + 1) % n_tx).start()
 
-    gain1, gain2, bias = [vecs[i:i + 1, :] for i in range(3)]
+    gain1, _, gain2, _, bias_o, bias_d = [vecs[i:i + 1, :] for i in range(6)]
+    bias = bias_o + bias_d
     turn = turn_tab[...]
 
     def rotate(v, sign):
-        return (v.astype(F32) * cos_tab[...] + sign * (dot_nn(v, turn) * sin_tab[...])).astype(BF16)
+        cos, sin = [jnp.concatenate([tab[...]] * (heads // 2), axis=1) for tab in (cos_tab, sin_tab)]
+        return (v.astype(F32) * cos + sign * (dot_nn(v, turn) * sin)).astype(BF16)
 
     def attend(s):
         slot = s % 2
@@ -535,7 +555,7 @@
     def forward_part(s):
         def body(r):
             at = block(r, blk)
-            total = dot_nt(u_b[at, :], w_d[...]) + dot_nt(ctx_s[at, :], w_a[:, 3 * width:])
+            total = dot_nn(u_b[at, :], w_d[...]) + dot_nt(ctx_s[at, :], w_a[:, 3 * width:])
             part[0, s % 2, at, :] = total.astype(BF16)
         loop(steps, body)
 
@@ -648,63 +668,60 @@
         for copy in load_late(s):
             copy.start()
         attend(s)
-        pl.when(s == 0)(lambda: rs_far(0))
-        pl.when(s == 2)(lambda: rs_far(1))
+        pl.when(s == 1)(lambda: rs_near(0))
+        pl.when(s == 2)(lambda: rs_near(1))
         for copy in load_late(s):
             copy.wait()
-
-        @pl.when(s == 2)
-        def _():
-            core_done(0)
-
+        pl.when(s == 2)(lambda: core_done(0))
         x_own[s % 2] = x_b[rows(t), :]
         c_own[s % 2] = cot_b[rows(t), :]
         forward_part(s)
         share(0, s)
         backward_part(s)
         share(1, s)
+        pl.when(s == 0)(lambda: rs_far(0))
         weight_part()
         give(s)
-
-        @pl.when(s == 0)
+        pl.when(s > 0)(lambda: finish(s - 1))
+
+        @pl.when(s == 1)
         def _():
-            rs_start(1)
-            rs_near(0)
-
-        @pl.when(s > 0)
-        def _():
-            finish(s - 1)
-
-        pl.when(s == 1)(lambda: rs_end(0))
-
-    rs_start(0)
+            rs_far(1)
+            rs_start(0, 0)
+
+        pl.when(s == 2)(lambda: rs_start(2, 2, 1))
+
+    for w in BOTH:
+        rs_start(w, 2, 1)
     loop(n_seq, one)
-    rs_start(2)
     forward(0)
-    rs_near(1)
     last = n_seq - 1
     MINE, CORE, PAIR, FROM_Y, QUAD = range(5)
-    sm_buf[MINE] = small[...]
+    sm_buf[MINE] = jnp.zeros_like(small_out)
+    sm_buf[MINE, 4:5, :], sm_buf[MINE, 6:7, :] = [jnp.sum(sums[i], axis=0, keepdims=True) for i in BOTH]
     for i in range(4):
         sm_buf[MINE, i:i + 1, :] = jnp.sum(ln_acc[i], axis=0, keepdims=True)
     sm_buf[MINE, 5:6, :3 * width] = jnp.sum(dbq[...], axis=0, keepdims=True)
     links.send(sm_slot[0], sm_buf.at[MINE], sm_buf.at[CORE], core_dev)
-    over_ty = (lax.broadcasted_iota(jnp.int32, small.shape, 0) < 4).astype(F32)
+    over_ty = (lax.broadcasted_iota(jnp.int32, small_out.shape, 0) < 4).astype(F32)
     finish(last)
+    rs_start(1, 0)
+    rs_start(2, 0)
     links.arrive(sm_slot[0], sm_buf.at[CORE], core_dev)
     sm_buf[PAIR] = sm_buf[MINE] + over_ty * sm_buf[CORE]
     links.send(sm_slot[PAIR], sm_buf.at[PAIR], sm_buf.at[FROM_Y], y_dev)
+    rs_end(0)
     forward(1)
     forward_y(0)
+    rs_far(2)
     links.arrive(sm_slot[PAIR], sm_buf.at[FROM_Y], y_dev)
     sm_buf[QUAD] = sm_buf[PAIR] + over_ty * sm_buf[FROM_Y]
     for k in OTHERS:
         links.send(sm_slot[QUAD + k], sm_buf.at[QUAD], sm_buf.at[QUAD + k], z_dev[k])
-    rs_far(2)
+    forward(last)
+    rs_near(2)
+    forward_y(1)
     rs_end(1)
-    forward(last)
-    forward_y(1)
-    rs_near(2)
     forward_y(last)
     rs_end(2)
     for k in OTHERS:
@@ -721,13 +738,13 @@
         links.sent(sm_slot[i], sm_buf.at[MINE])
 
 
-def layer_tail(qkv, d_ctx, u, d_pre, h1, x, cot, w_d, w_a, w_u, p_down, p_up, vecs, small, n_tx, n_ty):
+def layer_tail(qkv, d_ctx, u, d_pre, h1, x, cot, w_d, w_a, w_u, p_down, p_up, vecs, sums, n_tx, n_ty):
     n_seq, seq, d_model = x.shape
     end = n_tx - 1
     width, d_loc, blk, sub = d_ctx.shape[-1], d_model // n_tx, 256, seq // n_ty
     any_spec, vmem = pl.BlockSpec(memory_space=pl.ANY), pl.BlockSpec(memory_space=pltpu.VMEM)
     out = jax.ShapeDtypeStruct((n_seq * n_tx, seq, d_loc), BF16)
-    cos_tab, sin_tab = rope_tables(seq, width)
+    cos_tab, sin_tab = rope_tables(seq, 2 * HEAD)
     shapes = (p_down.shape[1:], p_up.shape[1:], (d_loc, d_model))
     slots = n_seq * 2 * (3 + 4 * n_tx) + 5 * 5
     wide = lambda *lead: pltpu.VMEM(lead + (seq, d_model), BF16)
@@ -736,7 +753,7 @@
         functools.partial(tail_kernel, n_tx=n_tx, blk=blk),
         in_specs=[any_spec] * 7 + [vmem] * 3 + [any_spec] * 2 + [vmem] * 5,
         out_specs=[any_spec] * 2 + [vmem] * 4,
-        out_shape=[out, out, *[jax.ShapeDtypeStruct(shape, F32) for shape in (small.shape, *shapes)]],
+        out_shape=[out, out, *[jax.ShapeDtypeStruct(shape, F32) for shape in (vecs.shape, *shapes)]],
         scratch_shapes=[
             pltpu.VMEM((2, seq, 3 * width), BF16),
             pltpu.VMEM((2, seq, width), BF16),
@@ -765,7 +782,7 @@
         compiler_params=pltpu.CompilerParams(collective_id=1, has_side_effects=True, vmem_limit_bytes=67_000_000),
         cost_estimate=pl.CostEstimate(flops=60_000_000_000, bytes_accessed=60_000_000, transcendentals=0),
         name="layer_tail",
-    )(qkv, d_ctx, u, d_pre, h1, x, cot, w_d, w_a, w_u, p_down, p_up, vecs, small, cos_tab, sin_tab, rope_turn(width))
+    )(qkv, d_ctx, u, d_pre, h1, x, cot, w_d, w_a, w_u, p_down, p_up, vecs, sums, cos_tab, sin_tab, rope_turn(width))
 
 
 def solution(mesh):
@@ -785,23 +802,16 @@
         z, g = lax.axis_index('tx'), lax.axis_index('dp')
 
         wq_loc = w_qkv.reshape(d_loc, heads, 3, HEAD).transpose(0, 2, 1, 3).reshape(d_loc, 3 * hw)
-        vec_loc = jnp.stack([ln1_gain, ln1_bias, ln2_gain, ln2_bias, b_dense, b_down], axis=0)
-        vec_loc = jnp.pad(vec_loc, ((0, 10), (0, 0)))
         bq = b_qkv.astype(F32).reshape(heads, 3, HEAD).transpose(1, 0, 2).reshape(1, 3 * hw)
-        x, cot, w_u, w_dt, w_a, vecs, h1, qkv, u, d_pre, d_ctx, part_down, part_up, d_bup = layer_front(
-            x_act, cot_out, w_up, w_down.T, jnp.concatenate([wq_loc, w_dense.T], axis=1), vec_loc, bq, b_up.astype(F32)[None], n_tx, n_ty)
-        g1, g2, b_o, b_d = [vecs[i].astype(F32) for i in (0, 2, 4, 5)]
-
-        d_b_up = d_bup.sum(0)
-        small = jnp.pad(d_b_up[None], ((4, 3), (0, d_model - d_b_up.shape[0])))
-        rows = jnp.pad(jnp.stack([g1, g2, b_o + b_d], axis=0), ((0, 5), (0, 0)))
+        x, cot, w_u, w_d, w_a, vecs, h1, qkv, u, d_pre, d_ctx, part_down, part_up, sums = layer_front(
+            x_act, cot_out, w_up, w_down, jnp.concatenate([wq_loc, w_dense.T], axis=1), (ln1_gain, ln1_bias, ln2_gain, ln2_bias, b_dense, b_down), bq, b_up, n_tx, n_ty)
         by_seq = lambda a: a.reshape(n_b, seq, a.shape[-1])
-        y_out, dx_act, total, d_w_down, d_w_up, d_w_a = layer_tail(by_seq(qkv), by_seq(d_ctx), by_seq(u), by_seq(d_pre), by_seq(h1), by_seq(x), by_seq(cot), w_dt, w_a, w_u, part_down, part_up, rows, small, n_tx, n_ty)
+        y_out, dx_act, total, d_w_down, d_w_up, d_w_a = layer_tail(by_seq(qkv), by_seq(d_ctx), by_seq(u), by_seq(d_pre), by_seq(h1), by_seq(x), by_seq(cot), w_d, w_a, w_u, part_down, part_up, vecs, sums, n_tx, n_ty)
         d_w_qkv = d_w_a[:, :3 * hw].reshape(d_loc, 3, heads, HEAD).transpose(0, 2, 1, 3).reshape(d_loc, heads, 3 * HEAD)
         d_w_dense = d_w_a[:, 3 * hw:].T
-        ln_sum = lax.dynamic_slice(total, (0, z * d_loc), (4, d_loc))
-        d_b_up, d_b_qkv = total[4, :d_b_up.shape[0]], total[5, :3 * hw].reshape(3, heads, HEAD).transpose(1, 0, 2).reshape(heads, 3 * HEAD)
-        d_b_out = cot_out.astype(F32).sum((0, 1))
-        return (y_out, dx_act, *ln_sum, d_w_qkv, d_b_qkv, d_w_dense, d_b_out, d_w_up, d_b_up, d_w_down, d_b_out)
+        by_width = lax.dynamic_slice(total, (0, z * d_loc), (8, d_loc))
+        d_b_up, d_b_qkv = total[4, :b_up.shape[0]], total[5, :3 * hw].reshape(3, heads, HEAD).transpose(1, 0, 2).reshape(heads, 3 * HEAD)
+        d_b_out = by_width[6]
+        return (y_out, dx_act, *by_width[:4], d_w_qkv, d_b_qkv, d_w_dense, d_b_out, d_w_up, d_b_up, d_w_down, d_b_out)
 
     return jax.shard_map(body, mesh=mesh, in_specs=in_specs, out_specs=out_specs, check_vma=False)

time: 336 us -> 322 us (0.958)
  the two profiles are of different devices: /device:TPU:0 before, /device:TPU:13 now
where the time goes in v2:
time: 322 us
  Pallas kernels  298 us (93%)
  local copies, waits for them, and re-layouts  22 us (7%)
    pallas_call x1, Pallas kernels, layer_tail(): pl.pallas_call(functools.partial(tail_kernel, n_tx=n_tx, blk=blk), in_spe...  169 us
    pallas_call x1, Pallas kernels, layer_front(): pl.pallas_call(functools.partial(front_kernel, n_tx=n_tx, n_ty=n_ty, blk=...  129 us
    unnamed x17, local copies, waits for them, and re-layouts  11.6 us

profile of v2, /device:TPU:13, one launch (start us, length us, event | category | flops | bytes accessed | tf_op | source)
XLA Modules:
  0.0 321.8 jit_solution(17514315274953197713)
XLA Ops:
  0.6 1.0 copy.43
  1.7 0.2 copy.45
  1.8 1.0 copy.44
  2.9 0.9 pad_maximum_fusion.wa_in
  3.7 0.8 reshape.100
  4.5 0.7 reshape.97.b_qkv
  5.2 129.4 %layer_front.1 = (bf16[2304,1024]{1,0:T(8,128)(2,1)}, bf16[2304,1024]{1,0:T(8,128)(2,1)}, bf16[1024,1024]{1,0:T(8,128)(2,1)}, bf16[1024,1024]{1,0:T(8,128)(2,1)}...) custom-call(bf16[4,4,576,256]{3,2,1,0:T(8,128)(2,1)} %bitcast.46, ...), custom_call_target="tpu_custom_call" | custom-call | flops 60000002048 | bytes 60000000 | tf_op jit(solution)/shard_map/layer_front/pallas_call | solution.py:354
  134.6 168.8 %layer_tail.1 = (bf16[12,768,256]{2,1,0:T(8,128)(2,1)}, bf16[12,768,256]{2,1,0:T(8,128)(2,1)}, f32[8,1024]{1,0:T(8,128)}, f32[1024,256]{1,0:T(8,128)}, f32[256,1024]{1,0:T(8,128)}, /*index=5*/f32[256,1024]{1,0:T(8,128)}) custom-call(bf16[3,768,768]{2,1,0:T(8,128)(2,1)} %bitcast.53, bf16[3,768,256]{2,1,0:T(8,128)(2,1)} %bitcast.54, ...), custom_call_target="tpu_custom_call" | custom-call | flops 60000002048 | bytes 60000000 | tf_op jit(solution)/shard_map/layer_tail/pallas_call | solution.py:752
  303.3 1.2 slice.20
  304.5 0.3 copy.47
  304.8 1.0 copy.48
  305.8 1.0 slice_bitcast_fusion
  306.7 0.0 slice-start
  306.8 0.8 copy.50
  307.6 0.8 slice_reduce_fusion
  308.3 0.1 reshape_squeeze.3
  308.4 0.7 reshape.95
  309.1 1.5 fusion
  310.6 0.0 copy-start.2
  310.6 1.4 slice.24
  312.0 0.6 copy.58
  312.6 0.0 slice-start.1
  312.6 5.0 %copy.59 = bf16[12,768,256]{2,1,0:T(8,128)(2,1)} copy(bf16[12,768,256]{2,1,0:T(8,128)(2,1)} %get-tuple-element.143) | data formatting | bytes 9437184
  317.5 0.0 copy-done.2
  317.5 0.0 slice-done
  317.5 0.0 slice-done.1
  317.5 0.0 copy-start.1
  317.6 0.0 copy-start
  317.6 2.3 copy.60
  319.9 0.0 copy-done.1
  319.9 1.0 copy.61
  320.8 0.0 copy-done
  320.8 1.0 copy.62
  (3 shorter events, 0.0 us)
Async XLA Ops:
  306.7 10.8 %slice-start = ((s8[4718592]{0:T(1024)(128)(4,1)}), s8[524288]{0:T(1024)(128)(4,1)S(1)}, s32[]{:S(2)}) async-start(s8[4718592]{0:T(1024)(128)(4,1)} %bitcast.30), calls=%async_computation | async-start | bytes 1048576
  310.6 6.9 %copy-start.2 = (f32[1,256]{1,0:T(1,128)}, f32[1,256]{1,0:T(1,128)S(1)}, u32[]{:S(2)}) copy-start(f32[1,256]{1,0:T(1,128)S(1)} %get-tuple-element.96) | copy-start | bytes 3076
  312.6 5.0 %slice-start.1 = ((s8[4718592]{0:T(1024)(128)(4,1)}), s8[4194304]{0:T(1024)(128)(4,1)S(1)}, s32[]{:S(2)}) async-start(s8[4718592]{0:T(1024)(128)(4,1)} %bitcast.30), calls=%async_computation.1 | async-start | bytes 8388608
  317.5 2.3 copy-start.1
  317.6 3.3 %copy-start = (f32[1024,256]{1,0:T(8,128)S(1)}, f32[1024,256]{1,0:T(8,128)}, u32[]{:S(2)}) copy-start(f32[1024,256]{1,0:T(8,128)} %get-tuple-element.155) | copy-start | bytes 3145732
